TPU v7x, 128 devices: a whole 4x4x4 slice. The times are simulated.
128 devices in a mesh: expert: 16 (over y_lo, x, core), row: 2 (over y_hi), col: 4 (over z).
Axes of the slice: x: 4, y: 4 (y_hi: 2, y_lo: 2; y = y_hi * 2 + y_lo), z: 4, core: 2. Of those that a mesh axis runs over, the one named last changes fastest.
Arguments:
- weights: bfloat16 [16, 4096, 7168], P('expert', 'row', 'col'), may hold values from -210 to 210
- inputs: bfloat16 [16, 1024, 4096], P('expert', ('row', 'col')), may hold values from -80 to 80
- cotangents: bfloat16 [16, 1024, 7168], P('expert', ('row', 'col')), may hold values from -150 to 150
- row_state: float32 [16, 4096], P('expert', 'row'), may hold values from 0.00089 to 0.91
- col_state: float32 [16, 7168], P('expert', 'col'), may hold values from 0.00089 to 0.91
Outputs:
- scaled_update: float32 [16, 4096, 7168], P('expert', 'row', 'col')
- new_row_state: float32 [16, 4096], P('expert', 'row')
- new_col_state: float32 [16, 7168], P('expert', 'col')
All inputs are finite; a program needn't handle non-finite values.
Results may differ from a plain program's by a relative error of at most 0.0003.
Values may be sent and summed in bfloat16 or wider, within the bound.
A program may use at most 128 MiB of HBM per device.

v0:
```python
import jax
import jax.numpy as jnp
from jax import lax
from jax.sharding import Mesh
from jax.sharding import PartitionSpec as P

STEP = 10
EXPERT_ROW_COL = ("expert_0", "expert_1", "expert_2", "row", "col")
EXPERT = ("expert_0", "expert_1", "expert_2")


eps_square = 1e-30


def laid_out(tiles, dim):
    lengths = list(tiles.shape[1:])
    lengths[dim] *= tiles.shape[0]
    return jnp.moveaxis(tiles, 0, dim).reshape(lengths)


def copy_for_each(array, axis):
    copies = jnp.broadcast_to(array, (lax.axis_size(axis), *array.shape))
    return lax.all_to_all(copies, axis, split_axis=0, concat_axis=0, tiled=True)


def gathered_copies(array, axis, dim):
    return laid_out(copy_for_each(array, axis), dim)


def by_axis(array, axes):
    for axis in axes:
        array = lax.psum(array, axis)
    return array


def of_everyone(array, axis):
    everything = copy_for_each(array, axis)
    return jnp.sum(everything, axis=0)


def together(arrays, axis):
    ends = [0]
    for a in arrays:
        ends.append(ends[-1] + a.size)
    so_far = of_everyone(jnp.concatenate([a.ravel() for a in arrays]), axis)
    return tuple((so_far[b:e].reshape(a.shape) for a, b, e in zip(arrays, ends, ends[1:])))


def reduce_factors(row_part, col_part):
    row_total = lax.psum(row_part, "col")
    col_total = lax.psum(col_part, "row")
    return (row_total, col_total)


def body(weights, inputs, cotangents, row_state, col_state):
    matrices, rows_here, cols_here = weights.shape
    model_width = inputs.shape[2]
    hidden_width = cotangents.shape[2]
    row_count = lax.axis_size("row")
    col_count = lax.axis_size("col")
    block_rows = inputs.shape[1]
    inputs_split = lax.all_to_all(inputs, "row", split_axis=2, concat_axis=1, tiled=True)
    hidden_split = lax.all_to_all(cotangents, "col", split_axis=2, concat_axis=1, tiled=True)
    hidden_all = gathered_copies(hidden_split, "row", 1)
    hidden_blocks = hidden_all.reshape(matrices, row_count, col_count, block_rows, cols_here)
    shard_rows = lax.all_gather(inputs_split, "col", axis=1, tiled=True)
    block_count = shard_rows.shape[1] // (row_count * block_rows)
    input_blocks = shard_rows.reshape(matrices, block_count, row_count, block_rows, rows_here)
    gradient = jnp.einsum(
        "mkrti,mrktj->mij", input_blocks, hidden_blocks, preferred_element_type=jnp.float32
    )
    decay_rate = 1.0 - STEP ** (-0.8)
    entry_count = model_width * hidden_width
    squares = gradient * gradient
    weights_wide = weights.astype(jnp.float32)
    weight_squares = jnp.sum(weights_wide * weights_wide, axis=(1, 2))
    squared_total = by_axis(jnp.sum(squares), EXPERT_ROW_COL)
    clip_scale = 1.0 / jnp.maximum(
        1.0, jnp.sqrt(squared_total / (matrices * lax.axis_size(EXPERT) * entry_count))
    )
    scale_square = clip_scale * clip_scale
    clipped = clip_scale * gradient
    row_raw, col_raw = reduce_factors(jnp.sum(squares, axis=2), jnp.sum(squares, axis=1))
    row_sum = row_raw * scale_square + hidden_width * eps_square
    col_sum = col_raw * scale_square + model_width * eps_square
    new_rows = decay_rate * row_state + (1.0 - decay_rate) * (row_sum / hidden_width)
    new_cols = decay_rate * col_state + (1.0 - decay_rate) * (col_sum / model_width)
    group_squares, old_rows, weight_total = together(
        (jnp.sum(squares, axis=(1, 2)), jnp.sum(row_state, axis=1), weight_squares), ("row", "col")
    )
    old_average = old_rows / (lax.axis_size("col") * model_width)
    fresh_average = group_squares * scale_square / entry_count + eps_square
    row_average = decay_rate * old_average + (1.0 - decay_rate) * fresh_average
    second = new_rows[:, :, None] * new_cols[:, None, :] / row_average[:, None, None]
    update = clipped / jnp.sqrt(second)
    update_squares = jnp.sum(update * update, axis=(1, 2))
    update_total = of_everyone(update_squares, ("row", "col"))
    update = update / jnp.maximum(1.0, jnp.sqrt(update_total / entry_count))[:, None, None]
    weight_rms = jnp.sqrt(weight_total / entry_count)
    return (weight_rms[:, None, None] * update, new_rows, new_cols)


def solution(mesh):
    split = Mesh(
        mesh.devices.reshape(2, 4, 2, mesh.shape["row"], mesh.shape["col"]),
        ("expert_0", "expert_1", "expert_2", "row", "col"),
    )
    return jax.shard_map(
        body,
        mesh=split,
        in_specs=(
            P(EXPERT, "row", "col"),
            P(EXPERT, ("row", "col"), None),
            P(EXPERT, ("row", "col"), None),
            P(EXPERT, "row"),
            P(EXPERT, "col"),
        ),
        out_specs=(P(EXPERT, "row", "col"), P(EXPERT, "row"), P(EXPERT, "col")),
        check_vma=False,
    )
```

profile of v0, /device:TPU:0, one launch (start us, length us, event | category | flops | bytes accessed | tf_op | source)
XLA Modules:
  0.0 310.9 jit_solution(1692544028264594254)
XLA Ops:
  7.2 5.0 %copy.36 = bf16[1,128,4096]{1,0,2:T(2,128)(2,1)S(1)} copy(bf16[1,128,4096]{2,1,0:T(8,128)(2,1)} %param.6) | data formatting | bytes 2097152 | tf_op args[1]
  12.8 22.4 %reduce.16 = bf16[4096,128]{1,0:T(8,128)(2,1)S(1)} reduce(bf16[4096,1,128]{2,1,0:T(2,128)(2,1)S(1)} %bitcast.45, bf16[]{:T(256)} %broadcast.24), dimensions={1}, to_apply=%bitcast.37.reduce_sub_computation | reduce | bytes 2097154
  35.5 19.5 %all_to_all.53 = bf16[2,2,131072]{2,1,0:T(2,128)(2,1)S(1)} all-to-all(bf16[2,2,131072]{2,1,0:T(2,128)(2,1)S(1)} %reshape.67), channel_id=1, replica_groups=mesh['expert_0'=2,'expert_1'=4,'expert_2'=2,'row'=2,'col'=4] {'row'}, dimensions={0} | all-to-all | bytes 2097152 | tf_op jit(solution)/shard_map/all_to_all | solution.py:62
  55.0 0.9 reshape.68
  56.0 1.4 copy.37
  57.4 8.6 %copy.38 = bf16[1,128,7168]{1,0,2:T(2,128)(2,1)} copy(bf16[1,128,7168]{2,1,0:T(8,128)(2,1)} %param.7) | data formatting | bytes 3670016 | tf_op args[2]
  66.0 41.1 %reduce.17 = bf16[7168,128]{1,0:T(8,128)(2,1)} reduce(bf16[7168,1,128]{2,1,0:T(2,128)(2,1)} %bitcast.42, bf16[]{:T(256)} %broadcast.24), dimensions={1}, to_apply=%bitcast.39.reduce_sub_computation | reduce | bytes 3670018
  107.1 2.5 reshape.69
  109.6 27.6 %all_to_all.54 = bf16[4,2,114688]{2,1,0:T(2,128)(2,1)} all-to-all(bf16[4,2,114688]{2,1,0:T(2,128)(2,1)S(1)} %reshape.69), channel_id=1, replica_groups=mesh['expert_0'=2,'expert_1'=4,'expert_2'=2,'row'=2,'col'=4] {'col'}, dimensions={0} | all-to-all | bytes 3670016 | tf_op jit(solution)/shard_map/all_to_all | solution.py:63
  137.1 4.7 %reshape.70 = bf16[7168,1,128]{2,1,0:T(2,128)(2,1)} reshape(bf16[4,2,114688]{2,1,0:T(2,128)(2,1)} %all_to_all.54) | data formatting | bytes 3670016
  141.8 2.3 copy.47
  144.1 2.4 copy.39
  146.6 1.7 broadcast_in_dim.6
  148.3 44.6 %all_to_all.55 = bf16[2,1,512,1792]{3,2,1,0:T(8,128)(2,1)} all-to-all(bf16[2,1,512,1792]{3,2,1,0:T(8,128)(2,1)S(1)} %broadcast_in_dim.6), channel_id=1, replica_groups=mesh['expert_0'=2,'expert_1'=4,'expert_2'=2,'row'=2,'col'=4] {'row'}, dimensions={0} | all-to-all | bytes 7340032 | tf_op jit(solution)/shard_map/all_to_all | solution.py:23
  192.9 16.7 %fusion.2 = (f32[2048]{0:T(1024)S(1)}, f32[1792]{0:T(1024)S(1)}, f32[]{:T(128)}, f32[2048,1792,1,1]{1,0,3,2:T(8,128)}) fusion(bf16[4,2,128,2048]{3,2,1,0:T(8,128)(2,1)} %bitcast.54, bf16[2,4,128,1792]{3,2,1,0:T(8,128)(2,1)} %bitcast.50), kind=kOutput, calls=%fused_computation.7 | convolution fusion | flops 7530868736 | bytes 22559748 | tf_op jit(solution)/shard_map/mkrti,mrktj->mij/dot_general | solution.py:69
  209.6 5.5 %psum.49 = f32[]{:T(128)} all-reduce(f32[]{:T(128)} %get-tuple-element.5), channel_id=1, replica_groups=mesh['expert_0'=2,'expert_1'=4,'expert_2'=2,'row'=2,'col'=4] {'expert_0'}, use_global_device_ids=true, to_apply=%region_4.0 | all-reduce | flops 1 | bytes 8 | tf_op jit(solution)/shard_map/psum | solution.py:32
  215.1 11.1 %psum.50 = f32[]{:T(128)} all-reduce(f32[]{:T(128)} %psum.49), channel_id=1, replica_groups=mesh['expert_0'=2,'expert_1'=4,'expert_2'=2,'row'=2,'col'=4] {'expert_1'}, use_global_device_ids=true, to_apply=%region_5.0 | all-reduce | flops 1 | bytes 8 | tf_op jit(solution)/shard_map/psum | solution.py:32
  226.2 3.1 psum.51
  229.3 7.5 %multiply_reduce_fusion.1 = f32[]{:T(128)} fusion(bf16[1,2048,1792]{2,1,0:T(8,128)(2,1)} %param.5), kind=kLoop, calls=%fused_computation.5 | loop fusion | flops 11010047 | bytes 7340036 | tf_op jit(solution)/shard_map/reduce_sum | solution.py:76
  236.7 7.1 %all-reduce.1 = (f32[]{:T(128)}, f32[1,1792]{1,0:T(1,128)S(1)}) all-reduce(f32[]{:T(128)} %psum.51, f32[1,1792]{1,0:T(1,128)S(1)} %reduce_sum.96), channel_id=1, replica_groups=mesh['expert_0'=2,'expert_1'=4,'expert_2'=2,'row'=2,'col'=4] {'row'}, use_global_device_ids=true, to_apply=%region_7.0 | all-reduce | flops 1793 | bytes 14344 | tf_op jit(solution)/shard_map/psum | solution.py:32
  243.8 9.7 %all-reduce = (f32[]{:T(128)}, f32[1,2048]{1,0:T(1,128)S(1)}) all-reduce(f32[]{:T(128)} %get-tuple-element.8, f32[1,2048]{1,0:T(1,128)S(1)} %bitcast.53), channel_id=1, replica_groups=mesh['expert_0'=2,'expert_1'=4,'expert_2'=2,'row'=2,'col'=4] {'col'}, use_global_device_ids=true, to_apply=%region_8.0 | all-reduce | flops 2049 | bytes 16392 | tf_op jit(solution)/shard_map/psum | solution.py:32
  254.3 0.7 multiply_add_fusion
  255.0 2.0 pad_maximum_fusion
  257.7 3.3 %all-to-all-start.3 = ((f32[8,1,3]{2,1,0:T(1,128)}), f32[8,1,3]{2,1,0:T(1,128)S(1)}, u32[]{:S(2)}, u32[]{:S(2)}) async-start(f32[8,1,3]{2,1,0:T(1,128)} %broadcast_in_dim.7), calls=%async_computation.3 | async-start | bytes 8192 | tf_op jit(solution)/shard_map/all_to_all | solution.py:23
  261.0 0.6 fusion.6
  261.6 7.0 %all-to-all-done.3 = f32[8,1,3]{2,1,0:T(1,128)S(1)} async-done(((f32[8,1,3]{2,1,0:T(1,128)}), f32[8,1,3]{2,1,0:T(1,128)S(1)}, u32[]{:S(2)}, u32[]{:S(2)}) %all-to-all-start.3) | async-done | bytes 128 | tf_op jit(solution)/shard_map/all_to_all | solution.py:23
  268.6 0.7 fusion.7
  271.3 8.9 %multiply_reduce_fusion = f32[]{:T(128)} fusion(f32[]{:T(128)} %bitcast.16, f32[1792]{0:T(1024)S(1)} %get-tuple-element.10, f32[2048]{0:T(1024)S(1)} %bitcast.51, f32[2048,1792,1,1]{1,0,3,2:T(8,128)} %get-tuple-element.17, f32[]{:T(128)S(6)} %div.45), kind=kLoop, calls=%fused_computation.4 | loop fusion | flops 22020096 | bytes 14695436 | tf_op jit(solution)/shard_map/reduce_sum | solution.py:96
  280.2 0.6 broadcast_in_dim.16
  280.8 10.1 %all_to_all.56 = f32[8,1,1]{2,1,0:T(1,128)S(1)} all-to-all(f32[8,1,1]{2,1,0:T(1,128)S(1)} %broadcast_in_dim.16), channel_id=1, replica_groups=mesh['expert_0'=2,'expert_1'=4,'expert_2'=2,'row'=2,'col'=4] {'row','col'}, dimensions={0} | all-to-all | bytes 64 | tf_op jit(solution)/shard_map/all_to_all | solution.py:23
  290.9 0.6 reduce_sum.98
  292.2 11.8 %multiply_bitcast_fusion = f32[1,2048,1792]{2,1,0:T(8,128)} fusion(f32[]{:T(128)S(6)} %max.8, f32[]{:T(128)} %bitcast.11, f32[]{:T(128)} %bitcast.16, f32[1792]{0:T(1024)S(1)} %get-tuple-element.10, f32[2048]{0:T(1024)S(1)} %bitcast.52, f32[2048,1792,1,1]{1,0,3,2:T(8,128)} %get-tuple-element.17, f32[]{:T(128)S(6)} %div.45), kind=kLoop, calls=%fused_computation.3 | loop fusion | flops 22020096 | bytes 29375504 | tf_op jit(solution)/shard_map/mul | solution.py:100
  (15 shorter events, 1.7 us)
Async XLA Ops:
  7.2 185.7 %all-gather.2.cloned.1.call-start = ((), (), s32[]{:S(2)}) async-start(), calls=%async_computation.5 | async-start | bytes 5242880 | tf_op jit(solution)/shard_map/all_gather | solution.py:66
  192.9 61.4 %copy-start.1 = (f32[1,2048]{1,0:T(1,128)S(1)}, f32[1,2048]{1,0:T(1,128)}, u32[]{:S(2)}) copy-start(f32[1,2048]{1,0:T(1,128)} %param.8) | copy-start | bytes 24580
  192.9 68.1 %copy-start.2 = (f32[1,1792]{1,0:T(1,128)S(1)}, f32[1,1792]{1,0:T(1,128)}, u32[]{:S(2)}) copy-start(f32[1,1792]{1,0:T(1,128)} %param.9) | copy-start | bytes 21508
  255.0 49.0 %copy-start = (f32[1,2048]{1,0:T(1,128)}, f32[1,2048]{1,0:T(1,128)S(1)}, u32[]{:S(2)}) copy-start(f32[1,2048]{1,0:T(1,128)S(1)} %get-tuple-element.12) | copy-start | bytes 24580
  257.7 11.0 %all-to-all-start.3 = ((f32[8,1,3]{2,1,0:T(1,128)}), f32[8,1,3]{2,1,0:T(1,128)S(1)}, u32[]{:S(2)}, u32[]{:S(2)}) async-start(f32[8,1,3]{2,1,0:T(1,128)} %broadcast_in_dim.7), calls=%async_computation.3 | async-start | bytes 8192 | tf_op jit(solution)/shard_map/all_to_all | solution.py:23
Sparse Core Ops, SparseCore 0:
  57.5 48.2 all-gather.1
where the time goes:
time: 312 us; the launch traced here: 311 us
  blocking collectives  138 us (44%)
  other arithmetic  95.6 us (31%)
  local copies, waits for them, and re-layouts  32.4 us (10%)
  between operations  17.5 us (6%)
  matrix products  16.7 us (5%)
  waiting for transfers between devices  7.01 us (2%)
  starting transfers between devices  3.37 us (1%)
    unnamed x2, other arithmetic  63.5 us
    all_to_all x2, blocking collectives, copy_for_each(): return lax.all_to_all(copies, axis, split_axis=0, concat_axis=0, tiled=True)  54.6 us
    psum x5, blocking collectives, by_axis(): array = lax.psum(array, axis)  36.6 us
    all_to_all x1, blocking collectives, body(): lax.all_to_all(cotangents, 'col', split_axis=2, concat_axis=1, tiled=True)  27.6 us
    unnamed x15, local copies, waits for them, and re-layouts  25 us
    all_to_all x1, blocking collectives, body(): lax.all_to_all(inputs, 'row', split_axis=2, concat_axis=1, tiled=True)  19.5 us
    dot_general x1, matrix products, body(): jnp.einsum('mkrti,mrktj->mij', input_blocks, hidden_blocks, preferred_ele...  16.7 us
    mul x1, other arithmetic, body(): return (weight_rms[:, None, None] * update, new_rows, new_cols)  11.8 us
  transfers between devices with their start and end apart: 2, of which 1 were waited for; matrix products, arithmetic and copies ran while one was open for 21% of the time, Pallas kernels for 0%

commit v1 on v0

v1 whole, which is shorter than its diff:
```python
import jax
import jax.numpy as jnp
from jax import lax
from jax.experimental import pallas as pl
from jax.experimental.pallas import tpu as pltpu
from jax.sharding import Mesh
from jax.sharding import PartitionSpec as P

STEP = 10
EPS = 1e-30
DECAY = 1.0 - STEP ** (-0.8)
EXPERT = ("ylo", "x", "core")
MESH = pl.DeviceIdType.MESH
F32 = jnp.float32
BF16 = jnp.bfloat16
SUBS = 4
LANES = 128
PLACE = (0, 1, 3, 2)


def neighbours():
    ylo, x, core = (lax.axis_index(a) for a in EXPERT)
    row, col = lax.axis_index("row"), lax.axis_index("col")
    group = []
    for dr in range(2):
        for dc in range(4):
            if dr or dc:
                place = {"row": lax.rem(row + dr, 2), "col": lax.rem(col + dc, 4)}
                group.append(((dr, dc), place))
    experts = []
    for dy in range(2):
        for dx in range(4):
            for dk in range(2):
                if dy or dx or dk:
                    place = {
                        "ylo": lax.rem(ylo + dy, 2),
                        "x": lax.rem(x + dx, 4),
                        "core": lax.rem(core + dk, 2),
                    }
                    experts.append(((dy, dx, dk), place))
    return dict(group), dict(experts)


def ring_sum(parts):
    return (parts[0] + parts[2]) + (parts[1] + parts[3])


def group_sum(parts):
    return ring_sum([parts[(0, c)] for c in range(4)]) + ring_sum([parts[(1, c)] for c in range(4)])


def full_sum(vector):
    return jnp.broadcast_to(jnp.sum(vector, keepdims=True), vector.shape)


def gather_kernel(
    weights, inputs, cotangents, row_state, col_state,
    grad, row_scale, col_scale, new_rows, new_cols,
    xg, yg, xt, xt_last, x_send, y_send, w_buf,
    w_acc, row_part, col_part, row_vec, col_vec, small,
    ring_rows, pair_cols, group_small, group_total, expert_total, update_part, group_update,
    local_sem, w_sem, yz_send, yz_recv, xz_send, xz_recv, fw_send, fw_recv, cross_send, cross_recv,
    r1_send, r1_recv, ex_send, ex_recv, r2_send, r2_recv,
):
    tokens = inputs.shape[1]
    rows, cols = grad.shape
    half, pair = rows // 2, 2 * tokens
    sub = half // SUBS
    row, col = lax.axis_index("row"), lax.axis_index("col")
    group, experts = neighbours()
    up, down, across = group[(0, 1)], group[(0, 3)], group[(0, 2)]
    partner = group[(1, 0)]

    def remote(src, dst, send, recv, device):
        return pltpu.make_async_remote_copy(
            src_ref=src, dst_ref=dst, send_sem=send, recv_sem=recv, device_id=device, device_id_type=MESH
        )

    def tokens_of(buffer, j, s, width=None):
        start = PLACE[j] * pair + s * tokens
        if width is None:
            return buffer.at[pl.ds(start, tokens)]
        return buffer.at[pl.ds(start, tokens), width]

    def row_cols(r):
        return pl.ds(pl.multiple_of(r * rows, rows), rows)

    def col_cols(c):
        return pl.ds(pl.multiple_of(c * cols, cols), cols)

    y_dest = (1, 3, 2)
    local = []
    for n, dc in enumerate(y_dest):
        local.append((cotangents.at[0, :, col_cols(lax.rem(col + dc, 4))], y_send.at[n]))
    local.append((inputs.at[0, :, row_cols(1 - row)], x_send))
    local.append((inputs.at[0, :, row_cols(row)], tokens_of(xg, 0, 0)))
    local.append((cotangents.at[0, :, col_cols(col)], tokens_of(yg, 0, 0)))
    loads = [pltpu.make_async_copy(s, d, local_sem.at[n]) for n, (s, d) in enumerate(local)]
    for n in (0, 1, 3, 4, 5, 2):
        loads[n].start()
    w_rows = w_buf.shape[1]
    w_steps = rows // w_rows

    def w_load(step, slot):
        start = pl.multiple_of(step * w_rows, w_rows)
        return pltpu.make_async_copy(weights.at[0, pl.ds(start, w_rows)], w_buf.at[slot], w_sem.at[slot])

    w_load(0, 0).start()

    barrier = pltpu.get_barrier_semaphore()
    everyone = [*group.values(), *experts.values()]
    for device in everyone:
        pl.semaphore_signal(barrier, inc=1, device_id=device, device_id_type=MESH)
    pl.semaphore_wait(barrier, len(everyone))

    y_copies = []
    for n, (dc, device) in enumerate(zip(y_dest, (up, down, across))):
        y_copies.append(
            remote(y_send.at[n], tokens_of(yg, (4 - dc) % 4, 0), yz_send.at[n], yz_recv.at[n], device)
        )
    lower, upper = pl.ds(0, half), pl.ds(half, half)

    def x_copy(s, direction, part):
        device, j = ((up, 3), (down, 1))[direction]
        width = (lower, upper)[direction ^ part]
        n = s * 4 + direction * 2 + part
        return remote(tokens_of(xg, 0, s, width), tokens_of(xg, j, s, width), xz_send.at[n], xz_recv.at[n], device)

    def forward(s, direction, step):
        device, j = ((up, 3), (down, 1))[direction]
        width = pl.ds(pl.multiple_of(direction * half + step * sub, LANES), sub)
        n = (s * 2 + direction) * SUBS + step
        return remote(tokens_of(xg, j, s, width), tokens_of(xg, 2, s, width), fw_send.at[n], fw_recv.at[n], device)

    cross_x = remote(x_send, tokens_of(xg, 0, 1), cross_send.at[4], cross_recv.at[4], partner)
    cross_y = [
        remote(tokens_of(yg, j, 0), tokens_of(yg, j, 1), cross_send.at[j], cross_recv.at[j], partner) for j in range(4)
    ]

    loads[0].wait()
    y_copies[0].start()
    loads[1].wait()
    y_copies[1].start()
    loads[3].wait()
    cross_x.start()
    loads[4].wait()
    for part in range(2):
        for direction in range(2):
            x_copy(0, direction, part).start()
    loads[5].wait()
    cross_y[0].start()
    loads[2].wait()
    y_copies[2].start()

    w_acc[...] = jnp.zeros_like(w_acc)

    @pl.loop(0, w_steps)
    def _(step):
        slot = lax.rem(step, 2)

        @pl.when(step + 1 < w_steps)
        def _():
            w_load(step + 1, 1 - slot).start()

        w_load(step, slot).wait()

        def add(i, total):
            block = w_buf[slot, pl.ds(pl.multiple_of(i * 16, 16), 16), :].astype(F32)
            block = block * block
            return total + (block[:8] + block[8:])

        w_acc[...] = lax.fori_loop(0, w_rows // 16, add, w_acc[...])

    weight_part = w_acc[:, :LANES]
    for n in range(1, cols // LANES):
        weight_part += w_acc[:, n * LANES : (n + 1) * LANES]
    small[8:16] = weight_part
    old_rows = row_state[...]
    small[16:24] = old_rows[:8] + old_rows[8:]

    def turn(first, count, start, width):
        @pl.loop(0, width // LANES)
        def _(i):
            at = pl.multiple_of(start + i * LANES, LANES)
            block = xg[first * pair : (first + count) * pair, pl.ds(at, LANES)]
            xt[pl.ds(at, LANES), first * pair : (first + count) * pair] = block.T

    n_width = 2 * LANES
    n_steps = cols // n_width

    def multiply(first, count, fresh):
        depth = slice(first * pair, (first + count) * pair)

        @pl.loop(0, n_steps)
        def _(n):
            at = pl.ds(pl.multiple_of(n * n_width, n_width), n_width)
            for m in range(2):
                part = jnp.dot(xt[m * half : (m + 1) * half, depth], yg[depth, at], preferred_element_type=F32)
                if not fresh:
                    part += grad[m * half : (m + 1) * half, at]
                grad[m * half : (m + 1) * half, at] = part

    y_copies[0].wait_recv()
    y_copies[1].wait_recv()
    cross_y[3].start()
    cross_y[1].start()
    cross_x.wait_recv()
    for part in range(2):
        for direction in range(2):
            x_copy(1, direction, part).start()
    turn(0, 1, 0, rows)
    cross_y[0].wait_recv()
    multiply(0, 1, True)
    y_copies[2].wait_recv()
    cross_y[2].start()

    for direction in range(2):
        x_copy(0, direction, 0).wait_recv()
    for direction in range(2):
        x_copy(1, direction, 0).wait_recv()
    for step in range(SUBS):
        for s in range(2):
            for direction in range(2):
                forward(s, direction, step).start()
    for s in range(2):
        for direction in range(2):
            x_copy(s, direction, 1).wait_recv()
    turn(1, 2, 0, rows)
    cross_y[3].wait_recv()
    cross_y[1].wait_recv()
    multiply(1, 2, False)
    cross_y[2].wait_recv()
    col_part[...] = jnp.zeros_like(col_part)

    last = slice(PLACE[2] * pair, (PLACE[2] + 1) * pair)

    @pl.loop(0, SUBS)
    def _(step):
        for s in range(2):
            for direction in range(2):
                forward(s, direction, step).wait_recv()
        starts = [pl.multiple_of(direction * half + step * sub, LANES) for direction in range(2)]
        for direction in range(2):
            for n in range(sub // LANES):
                at = pl.multiple_of(starts[direction] + n * LANES, LANES)
                to = direction * sub + n * LANES
                xt_last[to : to + LANES, :] = xg[last, pl.ds(at, LANES)].T
        row_part[...] = jnp.zeros_like(row_part)

        @pl.loop(0, n_steps)
        def _(n):
            at = pl.ds(pl.multiple_of(n * n_width, n_width), n_width)
            part = jnp.dot(xt_last[...], yg[last, at], preferred_element_type=F32)
            for direction in range(2):
                here = pl.ds(starts[direction], sub)
                block = part[direction * sub : (direction + 1) * sub] + grad[here, at]
                grad[here, at] = block
                block = block * block
                row_part[direction * sub : (direction + 1) * sub] += block[:, :LANES] + block[:, LANES:]
                col_part[:, at] += jnp.sum(block.reshape(sub // 8, 8, n_width), axis=0)

        for direction in range(2):
            for n in range(sub // LANES):
                to = direction * sub + n * LANES
                turned = row_part[to : to + LANES].T
                at = direction * (half // LANES) + step * (sub // LANES) + n
                row_vec[pl.ds(at, 1)] = jnp.sum(turned, axis=0, keepdims=True)

    col_vec[...] = jnp.sum(col_part[...], axis=0, keepdims=True)
    small[0:8] = row_vec[:8] + row_vec[8:]
    peers = list(group)
    r1 = []
    for dc in (1, 2, 3):
        r1.append(remote(row_vec, ring_rows.at[dc], r1_send.at[dc], r1_recv.at[dc], group[(0, (4 - dc) % 4)]))
    r1.append(remote(col_vec, pair_cols, r1_send.at[0], r1_recv.at[0], partner))
    for dr, dc in peers:
        n = dr * 4 + dc
        r1.append(
            remote(
                small, group_small.at[n], r1_send.at[4 + n], r1_recv.at[4 + n], group[(dr, (4 - dc) % 4)]
            )
        )
    for copy in r1[4:] + r1[:4]:
        copy.start()
    for copy in r1[4:]:
        copy.wait_recv()

    def of_group(part):
        parts = {(0, 0): small[part * 8 : part * 8 + 8]}
        for dr, dc in peers:
            parts[(dr, dc)] = group_small[dr * 4 + dc, part * 8 : part * 8 + 8]
        return parts

    squares = group_sum(of_group(0))
    group_total[...] = squares
    ex = []
    for n, (dy, dx, dk) in enumerate(experts):
        ex.append(
            remote(group_total, expert_total.at[n], ex_send.at[n], ex_recv.at[n], experts[(dy, (4 - dx) % 4, dk)])
        )
    for copy in ex:
        copy.start()
    weight_total = full_sum(group_sum(of_group(1)))
    old = of_group(2)
    old_total = full_sum(old[(0, 0)] + old[(1, 0)])
    group_squares = full_sum(squares)
    for copy in r1[:4]:
        copy.wait_recv()
    row_total = ring_sum([row_vec[...], ring_rows[1], ring_rows[2], ring_rows[3]])
    col_total = col_vec[...] + pair_cols[...]
    for copy in ex:
        copy.wait_recv()
    totals = {(0, 0, 0): squares}
    for n, key in enumerate(experts):
        totals[key] = expert_total[n]
    chips = [[totals[(dy, dx, 0)] + totals[(dy, dx, 1)] for dx in range(4)] for dy in range(2)]
    squared_total = full_sum(ring_sum(chips[0]) + ring_sum(chips[1]))

    model_width, hidden_width = 2 * rows, 4 * cols
    entries = model_width * hidden_width
    matrices = 1 + len(experts)
    clip = 1.0 / jnp.maximum(1.0, jnp.sqrt(squared_total / (matrices * entries)))
    clip_square = clip * clip
    row_square = jnp.concatenate([clip_square, clip_square], axis=0)
    fresh_rows = row_total * row_square + hidden_width * EPS
    fresh_cols = col_total * clip_square[:1, :1] + model_width * EPS
    rows_now = DECAY * row_state[...] + (1.0 - DECAY) * (fresh_rows / hidden_width)
    cols_now = DECAY * col_state[...] + (1.0 - DECAY) * (fresh_cols / model_width)
    new_rows[...] = rows_now
    new_cols[...] = cols_now
    average = DECAY * (old_total / model_width) + (1.0 - DECAY) * (group_squares * clip_square / entries + EPS)
    row_root = 1.0 / jnp.sqrt(rows_now)
    for n in range(rows // LANES):
        row_scale[n * LANES : (n + 1) * LANES] = jnp.broadcast_to(row_root[n : n + 1], (LANES, LANES)).T
    col_scale[...] = 1.0 / cols_now

    def weigh(i, total):
        here = pl.ds(pl.multiple_of(i * 32, 32), 32)
        line = None
        for n in range(cols // LANES):
            lane = slice(n * LANES, (n + 1) * LANES)
            block = grad[here, lane]
            block = block * block * col_scale[:, lane]
            line = block if line is None else line + block
        root = row_scale[here]
        line = line * root * root
        return total + ((line[0:8] + line[8:16]) + (line[16:24] + line[24:32]))

    update_part[...] = lax.fori_loop(0, rows // 32, weigh, jnp.zeros((8, LANES), F32))
    r2 = []
    for dr, dc in peers:
        n = dr * 4 + dc
        r2.append(
            remote(update_part, group_update.at[n], r2_send.at[n], r2_recv.at[n], group[(dr, (4 - dc) % 4)])
        )
    for copy in r2:
        copy.start()
    col_root = jnp.sqrt(col_scale[...])
    base = clip * jnp.sqrt(average) * jnp.sqrt(weight_total / entries)
    for copy in r2:
        copy.wait_recv()
    parts = {(0, 0): update_part[...]}
    for dr, dc in peers:
        parts[(dr, dc)] = group_update[dr * 4 + dc]
    update_total = full_sum(group_sum(parts)) * clip_square * average
    factor = base / jnp.maximum(1.0, jnp.sqrt(update_total / entries))
    col_scale[...] = col_root * factor[:1, :1]

    for copy in y_copies + [cross_x] + cross_y + r1 + ex + r2:
        copy.wait_send()
    for s in range(2):
        for direction in range(2):
            for part in range(2):
                x_copy(s, direction, part).wait_send()
            for step in range(SUBS):
                forward(s, direction, step).wait_send()


def scale_kernel(grad, row_scale, col_scale, rows_in, cols_in, out, rows_out, cols_out):
    step = pl.program_id(0)
    block = out.shape[0]

    @pl.when(step == 0)
    def _():
        rows_out[...] = rows_in[...]
        cols_out[...] = cols_in[...]

    @pl.loop(0, block // 8)
    def _(i):
        to = pl.ds(pl.multiple_of(i * 8, 8), 8)
        here = pl.ds(pl.multiple_of(step * block + i * 8, 8), 8)
        scale = row_scale[here]
        for n in range(out.shape[1] // LANES):
            lane = slice(n * LANES, (n + 1) * LANES)
            out[to, lane] = grad[here, lane] * scale * col_scale[:, lane]


def body(weights, inputs, cotangents, row_state, col_state):
    _, rows, cols = weights.shape
    tokens = inputs.shape[1]
    lines = rows // LANES
    vmem = pl.BlockSpec(memory_space=pltpu.VMEM)
    anywhere = pl.BlockSpec(memory_space=pl.ANY)
    shapes = [
        pltpu.VMEM((rows, cols), F32),
        pltpu.VMEM((rows, LANES), F32),
        pltpu.VMEM((1, cols), F32),
        pltpu.VMEM((lines, LANES), F32),
        pltpu.VMEM((1, cols), F32),
    ]
    sub = rows // 2 // SUBS
    dma = pltpu.SemaphoreType.DMA
    grad, row_scale, col_scale, new_rows, new_cols = pl.pallas_call(
        gather_kernel,
        name="gather_gradient",
        out_shape=shapes,
        in_specs=[anywhere, anywhere, anywhere, vmem, vmem],
        out_specs=[vmem] * 5,
        scratch_shapes=[
            pltpu.VMEM((8 * tokens, rows), BF16),
            pltpu.VMEM((8 * tokens, cols), BF16),
            pltpu.VMEM((rows, 6 * tokens), BF16),
            pltpu.VMEM((2 * sub, 2 * tokens), BF16),
            pltpu.VMEM((tokens, rows), BF16),
            pltpu.VMEM((3, tokens, cols), BF16),
            pltpu.VMEM((2, 256, cols), BF16),
            pltpu.VMEM((8, cols), F32),
            pltpu.VMEM((2 * sub, LANES), F32),
            pltpu.VMEM((8, cols), F32),
            pltpu.VMEM((lines, LANES), F32),
            pltpu.VMEM((1, cols), F32),
            pltpu.VMEM((24, LANES), F32),
            pltpu.VMEM((4, lines, LANES), F32),
            pltpu.VMEM((1, cols), F32),
            pltpu.VMEM((8, 24, LANES), F32),
            pltpu.VMEM((8, LANES), F32),
            pltpu.VMEM((15, 8, LANES), F32),
            pltpu.VMEM((8, LANES), F32),
            pltpu.VMEM((8, 8, LANES), F32),
            dma((6,)), dma((2,)), dma((3,)), dma((3,)), dma((8,)), dma((8,)),
            dma((4 * SUBS,)), dma((4 * SUBS,)), dma((5,)), dma((5,)),
            dma((12,)), dma((12,)), dma((15,)), dma((15,)), dma((8,)), dma((8,)),
        ],
        compiler_params=pltpu.CompilerParams(collective_id=0, has_side_effects=True, vmem_limit_bytes=44 * 2**20),
        cost_estimate=pl.CostEstimate(flops=16 * tokens * rows * cols, bytes_accessed=2**23, transcendentals=0),
    )(weights, inputs, cotangents, row_state.reshape(lines, LANES), col_state)
    steps = 8
    out, rows_out, cols_out = pl.pallas_call(
        scale_kernel,
        name="scale_update",
        grid=(steps,),
        out_shape=[
            jax.ShapeDtypeStruct((rows, cols), F32),
            jax.ShapeDtypeStruct((lines, LANES), F32),
            jax.ShapeDtypeStruct((1, cols), F32),
        ],
        in_specs=[vmem] * 5,
        out_specs=[
            pl.BlockSpec((rows // steps, cols), lambda i: (i, 0)),
            pl.BlockSpec((lines, LANES), lambda i: (0, 0)),
            pl.BlockSpec((1, cols), lambda i: (0, 0)),
        ],
        compiler_params=pltpu.CompilerParams(vmem_limit_bytes=10 * 2**20),
    )(grad, row_scale, col_scale, new_rows, new_cols)
    return out.reshape(1, rows, cols), rows_out.reshape(1, rows), cols_out


def solution(mesh):
    split = Mesh(
        mesh.devices.reshape(2, 4, 2, mesh.shape["row"], mesh.shape["col"]),
        (*EXPERT, "row", "col"),
    )
    return jax.shard_map(
        body,
        mesh=split,
        in_specs=(
            P(EXPERT, "row", "col"),
            P(EXPERT, ("row", "col"), None),
            P(EXPERT, ("row", "col"), None),
            P(EXPERT, "row"),
            P(EXPERT, "col"),
        ),
        out_specs=(P(EXPERT, "row", "col"), P(EXPERT, "row"), P(EXPERT, "col")),
        check_vma=False,
    )
```

time: 312 us -> 96.3 us (0.31)
  blocking collectives: 138 us -> 0 us
  other arithmetic: 95.6 us -> 0 us
  Pallas kernels: 0 us -> 95.3 us
  local copies, waits for them, and re-layouts: 32.4 us -> 0 us
  between operations: 17.5 us -> 0.64 us
  matrix products: 16.7 us -> 0 us
  waiting for transfers between devices: 7.01 us -> 0 us
  starting transfers between devices: 3.37 us -> 0 us
    all_to_all x4 -> x0, blocking collectives: 102 us -> none  [the longest x2 54.6 us: copy_for_each(): return lax.all_to_all(copies, axis, split_axis=0, concat_axis=0, tiled=True)]
    pallas_call x0 -> x2, Pallas kernels: none -> 95.3 us  [the longest x1 88.4 us: body(): pl.pallas_call(gather_kernel, name='gather_gradient', out_shape=shapes, i...]
    unnamed x2 -> x0, other arithmetic: 63.5 us -> none
    psum x5 -> x0, blocking collectives: 36.6 us -> none  [by_axis(): array = lax.psum(array, axis)]
    unnamed x15 -> x0, local copies, waits for them, and re-layouts: 25 us -> none
    reduce_sum x4 -> x0, other arithmetic: 17 us -> none  [the longest x1 8.87 us: body(): update_squares = jnp.sum(update * update, axis=(1, 2))]
    dot_general x1 -> x0, matrix products: 16.7 us -> none  [body(): jnp.einsum('mkrti,mrktj->mij', input_blocks, hidden_blocks, preferred_ele...]
    mul x1 -> x0, other arithmetic: 11.8 us -> none  [body(): return (weight_rms[:, None, None] * update, new_rows, new_cols)]
  transfers between devices with their start and end apart: 2 -> 0, of which waited for: 1 -> 0; matrix products, arithmetic and copies ran while one was open for 21% -> 0% of each run, Pallas kernels for 0% -> 0%
where the time goes in v1:
time: 96.3 us; the launch traced here: 96 us
  Pallas kernels  95.3 us (99%)
    pallas_call x1, Pallas kernels, body(): pl.pallas_call(gather_kernel, name='gather_gradient', out_shape=shapes, i...  88.4 us
    pallas_call x1, Pallas kernels, body(): pl.pallas_call(scale_kernel, name='scale_update', grid=(steps,), out_shap...  6.88 us

profile of v1, /device:TPU:0, one launch (start us, length us, event | category | flops | bytes accessed | tf_op | source)
XLA Modules:
  0.0 96.0 jit_solution(18125845939274601571)
XLA Ops:
  0.6 88.4 %gather_gradient.1 = (f32[2048,1792]{1,0:T(8,128)S(1)}, f32[2048,128]{1,0:T(8,128)S(1)}, f32[1,1792]{1,0:T(1,128)S(1)}, f32[16,128]{1,0:T(8,128)S(1)}, f32[1,1792]{1,0:T(1,128)S(1)}) custom-call(bf16[1,2048,1792]{2,1,0:T(8,128)(2,1)} %weights.1, bf16[1,128,4096]{2,1,0:T(8,128)(2,1)} %inputs.1, bf16[1,128,7168]{2,1,0:T(8,128)(2,1)} %cotangents.1, ...), custom_call_target="tpu_custom_call" | custom-call | flops 7516192768 | bytes 8388608 | tf_op jit(solution)/shard_map/gather_gradient/pallas_call | solution.py:413
  89.1 6.9 %scale_update.1 = (f32[2048,1792]{1,0:T(8,128)}, f32[16,128]{1,0:T(8,128)}, f32[1,1792]{1,0:T(1,128)}) custom-call(f32[2048,1792]{1,0:T(8,128)S(1)} %get-tuple-element.11.grad, f32[2048,128]{1,0:T(8,128)S(1)} %get-tuple-element.12.row_scale, f32[1,1792]{1,0:T(1,128)S(1)} %get-tuple-element.13.col_scale, f32[16,128]{1,0:T(8,128)S(1)} %get-tuple-element.14.rows_in, ...), custom_call_target="tpu_custom_call" | custom-call | tf_op jit(solution)/shard_map/scale_update/pallas_call | solution.py:448

commit v2 on v1

v2 whole, which is shorter than its diff:
```python
import jax
import jax.numpy as jnp
from jax import lax
from jax.experimental import pallas as pl
from jax.experimental.pallas import tpu as pltpu
from jax.sharding import Mesh
from jax.sharding import PartitionSpec as P

STEP = 10
EPS = 1e-30
DECAY = 1.0 - STEP ** (-0.8)
EXPERT = ("ylo", "x", "core")
MESH = pl.DeviceIdType.MESH
F32 = jnp.float32
BF16 = jnp.bfloat16
SUBS = 8
LANES = 128
PLACE = (0, 1, 3, 2)


def neighbours():
    ylo, x, core = (lax.axis_index(a) for a in EXPERT)
    row, col = lax.axis_index("row"), lax.axis_index("col")
    group = []
    for dr in range(2):
        for dc in range(4):
            if dr or dc:
                place = {"row": lax.rem(row + dr, 2), "col": lax.rem(col + dc, 4)}
                group.append(((dr, dc), place))
    experts = []
    for dy in range(2):
        for dx in range(4):
            for dk in range(2):
                if dy or dx or dk:
                    place = {
                        "ylo": lax.rem(ylo + dy, 2),
                        "x": lax.rem(x + dx, 4),
                        "core": lax.rem(core + dk, 2),
                    }
                    experts.append(((dy, dx, dk), place))
    return dict(group), dict(experts)


def ring_sum(parts):
    return (parts[0] + parts[2]) + (parts[1] + parts[3])


def group_sum(parts):
    return ring_sum([parts[(0, c)] for c in range(4)]) + ring_sum([parts[(1, c)] for c in range(4)])


def full_sum(vector):
    return jnp.broadcast_to(jnp.sum(vector, keepdims=True), vector.shape)


def gather_kernel(
    weights, inputs, cotangents, row_state_in, col_state_in,
    grad, row_scale, col_scale, new_rows, new_cols,
    xg, yg, xt, xt_last, x_send, y_send, w_buf, row_state, col_state,
    w_acc, squares, row_base, row_rate, row_part, col_part, row_vec, col_vec, small,
    ring_rows, pair_cols, group_small, group_total, expert_total, update_part, group_update,
    local_sem, w_sem, send_sem, yz_recv, xz_recv, fw_recv, cross_recv, sum_recv,
):
    tokens = inputs.shape[1]
    rows, cols = grad.shape
    half, pair = rows // 2, 2 * tokens
    sub = half // SUBS
    row, col = lax.axis_index("row"), lax.axis_index("col")
    group, experts = neighbours()
    up, down, across = group[(0, 1)], group[(0, 3)], group[(0, 2)]
    partner = group[(1, 0)]

    def remote(src, dst, send, recv, device):
        return pltpu.make_async_remote_copy(
            src_ref=src, dst_ref=dst, send_sem=send, recv_sem=recv, device_id=device, device_id_type=MESH
        )

    def tokens_of(buffer, j, s, width=None):
        start = PLACE[j] * pair + s * tokens
        if width is None:
            return buffer.at[pl.ds(start, tokens)]
        return buffer.at[pl.ds(start, tokens), width]

    def row_cols(r):
        return pl.ds(pl.multiple_of(r * rows, rows), rows)

    def col_cols(c):
        return pl.ds(pl.multiple_of(c * cols, cols), cols)

    y_dest = (1, 3, 2)
    local = []
    for n, dc in enumerate(y_dest):
        local.append((cotangents.at[0, :, col_cols(lax.rem(col + dc, 4))], y_send.at[n]))
    local.append((inputs.at[0, :, row_cols(1 - row)], x_send))
    local.append((inputs.at[0, :, row_cols(row)], tokens_of(xg, 0, 0)))
    local.append((cotangents.at[0, :, col_cols(col)], tokens_of(yg, 0, 0)))
    loads = [pltpu.make_async_copy(s, d, local_sem.at[n]) for n, (s, d) in enumerate(local)]
    loads.append(pltpu.make_async_copy(row_state_in, row_state, local_sem.at[6]))
    loads.append(pltpu.make_async_copy(col_state_in, col_state, local_sem.at[7]))
    for n in (0, 1, 3, 4, 5, 2, 6, 7):
        loads[n].start()
    w_rows = w_buf.shape[1]
    w_steps = rows // w_rows

    def w_load(step, slot):
        start = pl.multiple_of(step * w_rows, w_rows)
        return pltpu.make_async_copy(weights.at[0, pl.ds(start, w_rows)], w_buf.at[slot], w_sem.at[slot])

    w_load(0, 0).start()

    barrier = pltpu.get_barrier_semaphore()
    everyone = [*group.values(), *experts.values()]
    for device in everyone:
        pl.semaphore_signal(barrier, inc=1, device_id=device, device_id_type=MESH)
    pl.semaphore_wait(barrier, len(everyone))

    y_copies = []
    for n, (dc, device) in enumerate(zip(y_dest, (up, down, across))):
        y_copies.append(
            remote(y_send.at[n], tokens_of(yg, (4 - dc) % 4, 0), send_sem.at[0], yz_recv.at[n], device)
        )
    lower, upper = pl.ds(0, half), pl.ds(half, half)

    def x_copy(s, direction, part):
        device, j = ((up, 3), (down, 1))[direction]
        width = (lower, upper)[direction ^ part]
        recv = xz_recv.at[s * 2 + part]
        return remote(tokens_of(xg, 0, s, width), tokens_of(xg, j, s, width), send_sem.at[1], recv, device)

    def forward(s, direction, step):
        device, j = ((up, 3), (down, 1))[direction]
        width = pl.ds(direction * half + step * sub, sub)
        return remote(
            tokens_of(xg, j, s, width), tokens_of(xg, 2, s, width), send_sem.at[2], fw_recv.at[step], device
        )

    def await_bytes(like, sem):
        pltpu.make_async_copy(like, like, sem).wait()

    cross_x = remote(x_send, tokens_of(xg, 0, 1), send_sem.at[3], cross_recv.at[4], partner)
    cross_y = [
        remote(tokens_of(yg, j, 0), tokens_of(yg, j, 1), send_sem.at[4], cross_recv.at[j], partner) for j in range(4)
    ]

    loads[0].wait()
    y_copies[0].start()
    loads[1].wait()
    y_copies[1].start()
    loads[3].wait()
    cross_x.start()
    loads[4].wait()
    for part in range(2):
        for direction in range(2):
            x_copy(0, direction, part).start()
    loads[5].wait()
    cross_y[0].start()
    loads[2].wait()
    y_copies[2].start()

    w_acc[...] = jnp.zeros_like(w_acc)

    @pl.loop(0, w_steps)
    def _(step):
        slot = lax.rem(step, 2)

        @pl.when(step + 1 < w_steps)
        def _():
            w_load(step + 1, 1 - slot).start()

        w_load(step, slot).wait()

        def add(i, total):
            block = w_buf[slot, pl.ds(pl.multiple_of(i * 16, 16), 16), :].astype(F32)
            block = block * block
            return total + (block[:8] + block[8:])

        w_acc[...] = lax.fori_loop(0, w_rows // 16, add, w_acc[...])

    weight_part = w_acc[:, :LANES]
    for n in range(1, cols // LANES):
        weight_part += w_acc[:, n * LANES : (n + 1) * LANES]
    small[8:16] = weight_part
    loads[6].wait()
    loads[7].wait()
    old_rows = row_state[...]
    small[16:24] = old_rows[:8] + old_rows[8:]

    def turn(first, count, start, width):
        @pl.loop(0, width // LANES)
        def _(i):
            at = pl.multiple_of(start + i * LANES, LANES)
            block = xg[first * pair : (first + count) * pair, pl.ds(at, LANES)]
            xt[pl.ds(at, LANES), first * pair : (first + count) * pair] = block.T

    n_width = 2 * LANES
    n_steps = cols // n_width

    def multiply(place, halves, fresh=False):
        depth = slice(place * pair, (place + 1) * pair)

        @pl.loop(0, n_steps)
        def _(n):
            at = pl.ds(pl.multiple_of(n * n_width, n_width), n_width)
            for m in halves:
                here = slice(m * half, (m + 1) * half)
                part = jnp.dot(xt[here, depth], yg[depth, at], preferred_element_type=F32)
                if not fresh:
                    part += grad[here, at]
                grad[here, at] = part

    y_copies[0].wait_recv()
    y_copies[1].wait_recv()
    cross_y[3].start()
    cross_y[1].start()
    cross_x.wait_recv()
    for part in range(2):
        for direction in range(2):
            x_copy(1, direction, part).start()
    turn(0, 1, 0, rows)
    cross_y[0].wait_recv()
    multiply(0, (0, 1), fresh=True)
    y_copies[2].wait_recv()
    cross_y[2].start()

    await_bytes(x_send, xz_recv.at[0])
    await_bytes(x_send, xz_recv.at[2])
    for step in range(SUBS):
        for s in range(2):
            for direction in range(2):
                forward(s, direction, step).start()
    turn(2, 1, 0, half)
    turn(1, 1, half, half)
    cross_y[3].wait_recv()
    multiply(2, (0,))
    cross_y[1].wait_recv()
    multiply(1, (1,))
    await_bytes(x_send, xz_recv.at[1])
    await_bytes(x_send, xz_recv.at[3])
    turn(2, 1, half, half)
    turn(1, 1, 0, half)
    multiply(2, (1,))
    multiply(1, (0,))
    cross_y[2].wait_recv()
    col_part[...] = jnp.zeros_like(col_part)

    last = slice(PLACE[2] * pair, (PLACE[2] + 1) * pair)
    lanes = [slice(n * LANES, (n + 1) * LANES) for n in range(cols // LANES)]

    def finish(begin, width):
        starts = [pl.multiple_of(direction * half + begin, LANES) for direction in range(2)]
        for direction in range(2):
            for n in range(width // LANES):
                at = pl.multiple_of(starts[direction] + n * LANES, LANES)
                to = direction * width + n * LANES
                xt_last[to : to + LANES, :] = xg[last, pl.ds(at, LANES)].T

        @pl.loop(0, n_steps)
        def _(n):
            at = pl.ds(pl.multiple_of(n * n_width, n_width), n_width)
            part = jnp.dot(xt_last[: 2 * width], yg[last, at], preferred_element_type=F32)
            for direction in range(2):
                here = pl.ds(starts[direction], width)
                grad[here, at] = part[direction * width : (direction + 1) * width] + grad[here, at]

        for direction in range(2):

            def add(i, total):
                here = pl.ds(pl.multiple_of(starts[direction] + i * 8, 8), 8)
                line, out = None, []
                for lane, so_far in zip(lanes, total):
                    block = grad[here, lane]
                    block = block * block
                    squares[here, lane] = block
                    line = block if line is None else line + block
                    out.append(so_far + block)
                row_part[pl.ds(pl.multiple_of(direction * width + i * 8, 8), 8)] = line
                return tuple(out)

            total = lax.fori_loop(0, width // 8, add, tuple(col_part[:, lane] for lane in lanes), unroll=4)
            for lane, so_far in zip(lanes, total):
                col_part[:, lane] = so_far
            for n in range(width // LANES):
                to = direction * width + n * LANES
                turned = row_part[to : to + LANES].T
                at = (starts[direction] + n * LANES) // LANES
                row_vec[pl.ds(at, 1)] = jnp.sum(turned, axis=0, keepdims=True)

    def await_forward(step):
        await_bytes(x_send.at[:, pl.ds(0, 4 * sub)], fw_recv.at[step])

    double = SUBS // 2 - 1

    @pl.loop(0, double)
    def _(step):
        await_forward(2 * step)
        await_forward(2 * step + 1)
        finish(2 * step * sub, 2 * sub)

    @pl.loop(2 * double, SUBS)
    def _(step):
        await_forward(step)
        finish(step * sub, sub)

    col_vec[...] = jnp.sum(col_part[...], axis=0, keepdims=True)
    small[0:8] = row_vec[:8] + row_vec[8:]
    peers = list(group)
    for dr, dc in peers:
        n = dr * 4 + dc - 1
        remote(small, group_small.at[n], send_sem.at[5], sum_recv.at[0], group[(dr, (4 - dc) % 4)]).start()
    for dc in (1, 2, 3):
        remote(row_vec, ring_rows.at[dc - 1], send_sem.at[6], sum_recv.at[1], group[(0, (4 - dc) % 4)]).start()
    pair_copy = remote(col_vec, pair_cols, send_sem.at[7], sum_recv.at[2], partner)
    pair_copy.start()
    await_bytes(group_small, sum_recv.at[0])

    def of_group(part):
        parts = {(0, 0): small[part * 8 : part * 8 + 8]}
        for dr, dc in peers:
            parts[(dr, dc)] = group_small[dr * 4 + dc - 1, part * 8 : part * 8 + 8]
        return parts

    square_part = group_sum(of_group(0))
    group_total[...] = square_part
    for n, (dy, dx, dk) in enumerate(experts):
        remote(
            group_total, expert_total.at[n], send_sem.at[8], sum_recv.at[3], experts[(dy, (4 - dx) % 4, dk)]
        ).start()
    model_width, hidden_width = 2 * rows, 4 * cols
    entries = model_width * hidden_width
    matrices = 1 + len(experts)
    weight_total = full_sum(group_sum(of_group(1)))
    old = of_group(2)
    old_total = full_sum(old[(0, 0)] + old[(1, 0)])
    group_squares = full_sum(square_part)
    await_bytes(ring_rows, sum_recv.at[1])
    pair_copy.wait_recv()
    row_total = ring_sum([row_vec[...], ring_rows[0], ring_rows[1], ring_rows[2]])
    col_total = col_vec[...] + pair_cols[...]
    base = DECAY * row_state[...] + (1.0 - DECAY) * EPS
    rate = (1.0 - DECAY) * (row_total / hidden_width)
    for n in range(rows // LANES):
        here = slice(n * LANES, (n + 1) * LANES)
        row_base[here] = jnp.broadcast_to(base[n : n + 1], (LANES, LANES)).T
        row_rate[here] = jnp.broadcast_to(rate[n : n + 1], (LANES, LANES)).T
    await_bytes(expert_total, sum_recv.at[3])
    totals = {(0, 0, 0): square_part}
    for n, key in enumerate(experts):
        totals[key] = expert_total[n]
    chips = [[totals[(dy, dx, 0)] + totals[(dy, dx, 1)] for dx in range(4)] for dy in range(2)]
    squared_total = full_sum(ring_sum(chips[0]) + ring_sum(chips[1]))
    clip = 1.0 / jnp.maximum(1.0, jnp.sqrt(squared_total / (matrices * entries)))
    clip_square = clip * clip
    one = clip_square[:1, :1]
    fresh_cols = col_total * one + model_width * EPS
    cols_now = DECAY * col_state[...] + (1.0 - DECAY) * (fresh_cols / model_width)
    col_scale[...] = 1.0 / cols_now

    def weigh(i, total):
        here = pl.ds(pl.multiple_of(i * 64, 64), 64)
        line = None
        for lane in lanes:
            block = squares[here, lane] * col_scale[:, lane]
            line = block if line is None else line + block
        line = line / (row_base[here] + row_rate[here] * one)
        return total + jnp.sum(line.reshape(8, 8, LANES), axis=0)

    update_part[...] = lax.fori_loop(0, rows // 64, weigh, jnp.zeros((8, LANES), F32))
    for dr, dc in peers:
        n = dr * 4 + dc - 1
        remote(update_part, group_update.at[n], send_sem.at[9], sum_recv.at[4], group[(dr, (4 - dc) % 4)]).start()
    new_rows[...] = base + rate * one
    new_cols[...] = cols_now
    average = DECAY * (old_total / model_width) + (1.0 - DECAY) * (group_squares * clip_square / entries + EPS)

    @pl.loop(0, rows // 64)
    def _(i):
        here = pl.ds(pl.multiple_of(i * 64, 64), 64)
        row_scale[here] = 1.0 / jnp.sqrt(row_base[here] + row_rate[here] * one)

    col_root = jnp.sqrt(col_scale[...])
    scale = clip * jnp.sqrt(average) * jnp.sqrt(weight_total / entries)
    await_bytes(y_send, send_sem.at[0])
    await_bytes(xg.at[pl.ds(0, 4 * tokens)], send_sem.at[1])
    await_bytes(xg.at[pl.ds(0, 2 * tokens)], send_sem.at[2])
    cross_x.wait_send()
    await_bytes(yg.at[pl.ds(0, 4 * tokens)], send_sem.at[4])
    await_bytes(group_small, send_sem.at[5])
    await_bytes(ring_rows, send_sem.at[6])
    pair_copy.wait_send()
    await_bytes(expert_total, send_sem.at[8])
    await_bytes(group_update, send_sem.at[9])
    await_bytes(group_update, sum_recv.at[4])
    parts = {(0, 0): update_part[...]}
    for dr, dc in peers:
        parts[(dr, dc)] = group_update[dr * 4 + dc - 1]
    update_total = full_sum(group_sum(parts)) * clip_square * average
    factor = scale / jnp.maximum(1.0, jnp.sqrt(update_total / entries))
    col_scale[...] = col_root * factor[:1, :1]


def scale_kernel(grad, row_scale, col_scale, rows_in, cols_in, out, rows_out, cols_out, scaled, sem):
    rows, cols = grad.shape
    height = 64
    rows_copy = pltpu.make_async_copy(rows_in, rows_out, sem.at[1])
    cols_copy = pltpu.make_async_copy(cols_in, cols_out, sem.at[2])
    rows_copy.start()
    cols_copy.start()

    @pl.loop(0, rows // height)
    def _(step):
        for i in range(height // 8):
            here = pl.ds(pl.multiple_of(step * height + i * 8, 8), 8)
            scale = row_scale[here]
            for n in range(cols // LANES):
                lane = slice(n * LANES, (n + 1) * LANES)
                scaled[here, lane] = grad[here, lane] * scale * col_scale[:, lane]
        block = pl.ds(pl.multiple_of(step * height, height), height)
        pltpu.make_async_copy(scaled.at[block], out.at[block], sem.at[0]).start()

    rows_copy.wait()
    cols_copy.wait()
    pltpu.make_async_copy(scaled, out, sem.at[0]).wait()


def body(weights, inputs, cotangents, row_state, col_state):
    _, rows, cols = weights.shape
    tokens = inputs.shape[1]
    lines = rows // LANES
    vmem = pl.BlockSpec(memory_space=pltpu.VMEM)
    anywhere = pl.BlockSpec(memory_space=pl.ANY)
    shapes = [
        pltpu.VMEM((rows, cols), F32),
        pltpu.VMEM((rows, LANES), F32),
        pltpu.VMEM((1, cols), F32),
        pltpu.VMEM((lines, LANES), F32),
        pltpu.VMEM((1, cols), F32),
    ]
    sub = rows // 2 // SUBS
    dma = pltpu.SemaphoreType.DMA
    grad, row_scale, col_scale, new_rows, new_cols = pl.pallas_call(
        gather_kernel,
        name="gather_gradient",
        out_shape=shapes,
        in_specs=[anywhere] * 5,
        out_specs=[vmem] * 5,
        scratch_shapes=[
            pltpu.VMEM((8 * tokens, rows), BF16),
            pltpu.VMEM((8 * tokens, cols), BF16),
            pltpu.VMEM((rows, 6 * tokens), BF16),
            pltpu.VMEM((4 * sub, 2 * tokens), BF16),
            pltpu.VMEM((tokens, rows), BF16),
            pltpu.VMEM((3, tokens, cols), BF16),
            pltpu.VMEM((2, 256, cols), BF16),
            pltpu.VMEM((lines, LANES), F32),
            pltpu.VMEM((1, cols), F32),
            pltpu.VMEM((8, cols), F32),
            pltpu.VMEM((rows, cols), F32),
            pltpu.VMEM((rows, LANES), F32),
            pltpu.VMEM((rows, LANES), F32),
            pltpu.VMEM((4 * sub, LANES), F32),
            pltpu.VMEM((8, cols), F32),
            pltpu.VMEM((lines, LANES), F32),
            pltpu.VMEM((1, cols), F32),
            pltpu.VMEM((24, LANES), F32),
            pltpu.VMEM((3, lines, LANES), F32),
            pltpu.VMEM((1, cols), F32),
            pltpu.VMEM((7, 24, LANES), F32),
            pltpu.VMEM((8, LANES), F32),
            pltpu.VMEM((15, 8, LANES), F32),
            pltpu.VMEM((8, LANES), F32),
            pltpu.VMEM((7, 8, LANES), F32),
            dma((8,)), dma((2,)), dma((10,)), dma((3,)), dma((4,)), dma((SUBS,)), dma((5,)), dma((5,)),
        ],
        compiler_params=pltpu.CompilerParams(collective_id=0, has_side_effects=True, vmem_limit_bytes=40 * 2**20),
        cost_estimate=pl.CostEstimate(flops=16 * tokens * rows * cols, bytes_accessed=2**23, transcendentals=0),
    )(weights, inputs, cotangents, row_state.reshape(lines, LANES), col_state)
    out, rows_out, cols_out = pl.pallas_call(
        scale_kernel,
        name="scale_update",
        out_shape=[
            jax.ShapeDtypeStruct((rows, cols), F32),
            jax.ShapeDtypeStruct((lines, LANES), F32),
            jax.ShapeDtypeStruct((1, cols), F32),
        ],
        in_specs=[vmem] * 5,
        out_specs=[anywhere] * 3,
        scratch_shapes=[pltpu.VMEM((rows, cols), F32), dma((3,))],
        compiler_params=pltpu.CompilerParams(vmem_limit_bytes=20 * 2**20),
    )(grad, row_scale, col_scale, new_rows, new_cols)
    return out.reshape(1, rows, cols), rows_out.reshape(1, rows), cols_out


def solution(mesh):
    split = Mesh(
        mesh.devices.reshape(2, 4, 2, mesh.shape["row"], mesh.shape["col"]),
        (*EXPERT, "row", "col"),
    )
    return jax.shard_map(
        body,
        mesh=split,
        in_specs=(
            P(EXPERT, "row", "col"),
            P(EXPERT, ("row", "col"), None),
            P(EXPERT, ("row", "col"), None),
            P(EXPERT, "row"),
            P(EXPERT, "col"),
        ),
        out_specs=(P(EXPERT, "row", "col"), P(EXPERT, "row"), P(EXPERT, "col")),
        check_vma=False,
    )
```

time: 96.3 us -> 95.1 us (0.988)
  Pallas kernels: 95.3 us -> 94.1 us
    pallas_call x1, Pallas kernels: 6.88 us -> 5.26 us  [body(): pl.pallas_call(scale_kernel, name='scale_update', out_shape=[jax.ShapeDty...]
where the time goes in v2:
time: 95.1 us; the launch traced here: 94.7 us
  Pallas kernels  94.1 us (99%)
    pallas_call x1, Pallas kernels, body(): pl.pallas_call(gather_kernel, name='gather_gradient', out_shape=shapes, i...  88.8 us
    pallas_call x1, Pallas kernels, body(): pl.pallas_call(scale_kernel, name='scale_update', out_shape=[jax.ShapeDty...  5.26 us

profile of v2, /device:TPU:0, one launch (start us, length us, event | category | flops | bytes accessed | tf_op | source)
XLA Modules:
  0.0 94.7 jit_solution(7034354266929041817)
XLA Ops:
  0.6 88.8 %gather_gradient.1 = (f32[2048,1792]{1,0:T(8,128)S(1)}, f32[2048,128]{1,0:T(8,128)S(1)}, f32[1,1792]{1,0:T(1,128)S(1)}, f32[16,128]{1,0:T(8,128)S(1)}, f32[1,1792]{1,0:T(1,128)S(1)}) custom-call(bf16[1,2048,1792]{2,1,0:T(8,128)(2,1)} %weights.1, bf16[1,128,4096]{2,1,0:T(8,128)(2,1)} %inputs.1, bf16[1,128,7168]{2,1,0:T(8,128)(2,1)} %cotangents.1, ...), custom_call_target="tpu_custom_call" | custom-call | flops 7516192768 | bytes 8388608 | tf_op jit(solution)/shard_map/gather_gradient/pallas_call | solution.py:440
  89.5 5.3 %scale_update.1 = (f32[2048,1792]{1,0:T(8,128)}, f32[16,128]{1,0:T(8,128)}, f32[1,1792]{1,0:T(1,128)}) custom-call(f32[2048,1792]{1,0:T(8,128)S(1)} %get-tuple-element.11.grad, f32[2048,128]{1,0:T(8,128)S(1)} %get-tuple-element.12.row_scale, f32[1,1792]{1,0:T(1,128)S(1)} %get-tuple-element.13.col_scale, f32[16,128]{1,0:T(8,128)S(1)} %get-tuple-element.14.rows_in, ...), custom_call_target="tpu_custom_call" | custom-call | tf_op jit(solution)/shard_map/scale_update/pallas_call | solution.py:477

commit v3 on v2

--- a/solution.py
+++ b/solution.py
@@ -15,6 +15,7 @@
 BF16 = jnp.bfloat16
 SUBS = 8
 LANES = 128
+LAST_STEPS = ((0, 3), (3, 6), (6, 7))
 PLACE = (0, 1, 3, 2)
 
 
@@ -138,9 +139,16 @@
         pltpu.make_async_copy(like, like, sem).wait()
 
     cross_x = remote(x_send, tokens_of(xg, 0, 1), send_sem.at[3], cross_recv.at[4], partner)
-    cross_y = [
-        remote(tokens_of(yg, j, 0), tokens_of(yg, j, 1), send_sem.at[4], cross_recv.at[j], partner) for j in range(4)
-    ]
+    cross_y = {
+        j: remote(tokens_of(yg, j, 0), tokens_of(yg, j, 1), send_sem.at[4], cross_recv.at[j], partner) for j in (0, 1, 3)
+    }
+    n_width = 2 * LANES
+    n_steps = cols // n_width
+    cross_last = []
+    for n, (first, end) in enumerate(LAST_STEPS):
+        width = pl.ds(first * n_width, (end - first) * n_width)
+        recv = cross_recv.at[5 + n]
+        cross_last.append(remote(tokens_of(yg, 2, 0, width), tokens_of(yg, 2, 1, width), send_sem.at[4], recv, partner))
 
     loads[0].wait()
     y_copies[0].start()
@@ -192,15 +200,11 @@
             block = xg[first * pair : (first + count) * pair, pl.ds(at, LANES)]
             xt[pl.ds(at, LANES), first * pair : (first + count) * pair] = block.T
 
-    n_width = 2 * LANES
-    n_steps = cols // n_width
-
     def multiply(place, halves, fresh=False):
         depth = slice(place * pair, (place + 1) * pair)
 
-        @pl.loop(0, n_steps)
-        def _(n):
-            at = pl.ds(pl.multiple_of(n * n_width, n_width), n_width)
+        for n in range(n_steps):
+            at = slice(n * n_width, (n + 1) * n_width)
             for m in halves:
                 here = slice(m * half, (m + 1) * half)
                 part = jnp.dot(xt[here, depth], yg[depth, at], preferred_element_type=F32)
@@ -220,7 +224,8 @@
     cross_y[0].wait_recv()
     multiply(0, (0, 1), fresh=True)
     y_copies[2].wait_recv()
-    cross_y[2].start()
+    for copy in cross_last:
+        copy.start()
 
     await_bytes(x_send, xz_recv.at[0])
     await_bytes(x_send, xz_recv.at[2])
@@ -240,73 +245,83 @@
     turn(1, 1, 0, half)
     multiply(2, (1,))
     multiply(1, (0,))
-    cross_y[2].wait_recv()
     col_part[...] = jnp.zeros_like(col_part)
-
     last = slice(PLACE[2] * pair, (PLACE[2] + 1) * pair)
     lanes = [slice(n * LANES, (n + 1) * LANES) for n in range(cols // LANES)]
 
-    def finish(begin, width):
-        starts = [pl.multiple_of(direction * half + begin, LANES) for direction in range(2)]
-        for direction in range(2):
-            for n in range(width // LANES):
-                at = pl.multiple_of(starts[direction] + n * LANES, LANES)
-                to = direction * width + n * LANES
-                xt_last[to : to + LANES, :] = xg[last, pl.ds(at, LANES)].T
-
-        @pl.loop(0, n_steps)
-        def _(n):
-            at = pl.ds(pl.multiple_of(n * n_width, n_width), n_width)
-            part = jnp.dot(xt_last[: 2 * width], yg[last, at], preferred_element_type=F32)
-            for direction in range(2):
-                here = pl.ds(starts[direction], width)
-                grad[here, at] = part[direction * width : (direction + 1) * width] + grad[here, at]
-
-        for direction in range(2):
-
-            def add(i, total):
-                here = pl.ds(pl.multiple_of(starts[direction] + i * 8, 8), 8)
-                line, out = None, []
-                for lane, so_far in zip(lanes, total):
-                    block = grad[here, lane]
-                    block = block * block
-                    squares[here, lane] = block
-                    line = block if line is None else line + block
-                    out.append(so_far + block)
-                row_part[pl.ds(pl.multiple_of(direction * width + i * 8, 8), 8)] = line
-                return tuple(out)
-
-            total = lax.fori_loop(0, width // 8, add, tuple(col_part[:, lane] for lane in lanes), unroll=4)
-            for lane, so_far in zip(lanes, total):
-                col_part[:, lane] = so_far
-            for n in range(width // LANES):
-                to = direction * width + n * LANES
-                turned = row_part[to : to + LANES].T
-                at = (starts[direction] + n * LANES) // LANES
-                row_vec[pl.ds(at, 1)] = jnp.sum(turned, axis=0, keepdims=True)
-
     def await_forward(step):
         await_bytes(x_send.at[:, pl.ds(0, 4 * sub)], fw_recv.at[step])
-
-    double = SUBS // 2 - 1
-
-    @pl.loop(0, double)
-    def _(step):
-        await_forward(2 * step)
-        await_forward(2 * step + 1)
-        finish(2 * step * sub, 2 * sub)
-
-    @pl.loop(2 * double, SUBS)
-    def _(step):
-        await_forward(step)
-        finish(step * sub, sub)
-
-    col_vec[...] = jnp.sum(col_part[...], axis=0, keepdims=True)
-    small[0:8] = row_vec[:8] + row_vec[8:]
+        for direction in range(2):
+            at = direction * half + step * sub
+            to = (2 * step + direction) * sub
+            xt_last[to : to + sub, :] = xg[last, at : at + sub].T
+
+    def finish(first, end, steps):
+        for n in range(*steps):
+            at = slice(n * n_width, (n + 1) * n_width)
+            part = jnp.dot(xt_last[first * 2 * sub : end * 2 * sub], yg[last, at], preferred_element_type=F32)
+            total = col_part[:, at]
+            for step in range(first, end):
+                for direction in range(2):
+                    here = slice(direction * half + step * sub, direction * half + (step + 1) * sub)
+                    begin = (2 * (step - first) + direction) * sub
+                    block = part[begin : begin + sub] + grad[here, at]
+                    grad[here, at] = block
+                    block = block * block
+                    total += jnp.sum(block.reshape(sub // 8, 8, n_width), axis=0)
+            col_part[:, at] = total
+
+    def square(first, width):
+        for direction in range(2):
+
+            @pl.loop(0, width // 32)
+            def _(i):
+                for k in range(4):
+                    begin = direction * half + first + i * 32 + k * 8
+                    here = pl.ds(pl.multiple_of(begin, 8), 8)
+                    line = None
+                    for lane in lanes:
+                        block = grad[here, lane]
+                        block = block * block
+                        squares[here, lane] = block
+                        line = block if line is None else line + block
+                    row_part[here] = line
+
+            for n in range(width // LANES):
+                begin = direction * half + first + n * LANES
+                turned = row_part[begin : begin + LANES].T
+                row_vec[begin // LANES : begin // LANES + 1] = jnp.sum(turned, axis=0, keepdims=True)
+
+    await_forward(0)
+    await_forward(1)
+    cross_last[0].wait_recv()
+    finish(0, 2, LAST_STEPS[0])
+    await_forward(2)
+    await_forward(3)
+    finish(2, 4, LAST_STEPS[0])
+    cross_last[1].wait_recv()
+    finish(0, 4, LAST_STEPS[1])
+    await_forward(4)
+    await_forward(5)
+    finish(4, 6, (0, LAST_STEPS[1][1]))
+    cross_last[2].wait_recv()
+    finish(0, 6, LAST_STEPS[2])
+    await_forward(6)
+    finish(6, 7, (0, n_steps))
+    square(0, 2 * sub)
+    await_forward(7)
+    finish(7, 8, (0, n_steps))
+
+    square_part = col_part[:, :LANES]
+    for lane in lanes[1:]:
+        square_part += col_part[:, lane]
+    small[0:8] = square_part
     peers = list(group)
     for dr, dc in peers:
         n = dr * 4 + dc - 1
         remote(small, group_small.at[n], send_sem.at[5], sum_recv.at[0], group[(dr, (4 - dc) % 4)]).start()
+    col_vec[...] = jnp.sum(col_part[...], axis=0, keepdims=True)
+    square(2 * sub, 6 * sub)
     for dc in (1, 2, 3):
         remote(row_vec, ring_rows.at[dc - 1], send_sem.at[6], sum_recv.at[1], group[(0, (4 - dc) % 4)]).start()
     pair_copy = remote(col_vec, pair_cols, send_sem.at[7], sum_recv.at[2], partner)
@@ -447,7 +462,7 @@
             pltpu.VMEM((8 * tokens, rows), BF16),
             pltpu.VMEM((8 * tokens, cols), BF16),
             pltpu.VMEM((rows, 6 * tokens), BF16),
-            pltpu.VMEM((4 * sub, 2 * tokens), BF16),
+            pltpu.VMEM((rows, 2 * tokens), BF16),
             pltpu.VMEM((tokens, rows), BF16),
             pltpu.VMEM((3, tokens, cols), BF16),
             pltpu.VMEM((2, 256, cols), BF16),
@@ -457,7 +472,7 @@
             pltpu.VMEM((rows, cols), F32),
             pltpu.VMEM((rows, LANES), F32),
             pltpu.VMEM((rows, LANES), F32),
-            pltpu.VMEM((4 * sub, LANES), F32),
+            pltpu.VMEM((rows, LANES), F32),
             pltpu.VMEM((8, cols), F32),
             pltpu.VMEM((lines, LANES), F32),
             pltpu.VMEM((1, cols), F32),
@@ -469,7 +484,7 @@
             pltpu.VMEM((15, 8, LANES), F32),
             pltpu.VMEM((8, LANES), F32),
             pltpu.VMEM((7, 8, LANES), F32),
-            dma((8,)), dma((2,)), dma((10,)), dma((3,)), dma((4,)), dma((SUBS,)), dma((5,)), dma((5,)),
+            dma((8,)), dma((2,)), dma((10,)), dma((3,)), dma((4,)), dma((SUBS,)), dma((8,)), dma((5,)),
         ],
         compiler_params=pltpu.CompilerParams(collective_id=0, has_side_effects=True, vmem_limit_bytes=40 * 2**20),
         cost_estimate=pl.CostEstimate(flops=16 * tokens * rows * cols, bytes_accessed=2**23, transcendentals=0),

time: 95.1 us -> 87.8 us (0.923)
  Pallas kernels: 94.1 us -> 86.4 us
    pallas_call x1, Pallas kernels: 88.8 us -> 81.1 us  [body(): pl.pallas_call(gather_kernel, name='gather_gradient', out_shape=shapes, i...]
where the time goes in v3:
time: 87.8 us; the launch traced here: 87.2 us
  Pallas kernels  86.4 us (98%)
    pallas_call x1, Pallas kernels, body(): pl.pallas_call(gather_kernel, name='gather_gradient', out_shape=shapes, i...  81.1 us
    pallas_call x1, Pallas kernels, body(): pl.pallas_call(scale_kernel, name='scale_update', out_shape=[jax.ShapeDty...  5.26 us

profile of v3, /device:TPU:0, one launch (start us, length us, event | category | flops | bytes accessed | tf_op | source)
XLA Modules:
  0.0 87.2 jit_solution(7456497004400720555)
XLA Ops:
  0.6 81.1 %gather_gradient.1 = (f32[2048,1792]{1,0:T(8,128)S(1)}, f32[2048,128]{1,0:T(8,128)S(1)}, f32[1,1792]{1,0:T(1,128)S(1)}, f32[16,128]{1,0:T(8,128)S(1)}, f32[1,1792]{1,0:T(1,128)S(1)}) custom-call(bf16[1,2048,1792]{2,1,0:T(8,128)(2,1)} %weights.1, bf16[1,128,4096]{2,1,0:T(8,128)(2,1)} %inputs.1, bf16[1,128,7168]{2,1,0:T(8,128)(2,1)} %cotangents.1, ...), custom_call_target="tpu_custom_call" | custom-call | flops 7516192768 | bytes 8388608 | tf_op jit(solution)/shard_map/gather_gradient/pallas_call | solution.py:455
  81.8 5.3 %scale_update.1 = (f32[2048,1792]{1,0:T(8,128)}, f32[16,128]{1,0:T(8,128)}, f32[1,1792]{1,0:T(1,128)}) custom-call(f32[2048,1792]{1,0:T(8,128)S(1)} %get-tuple-element.11.grad, f32[2048,128]{1,0:T(8,128)S(1)} %get-tuple-element.12.row_scale, f32[1,1792]{1,0:T(1,128)S(1)} %get-tuple-element.13.col_scale, f32[16,128]{1,0:T(8,128)S(1)} %get-tuple-element.14.rows_in, ...), custom_call_target="tpu_custom_call" | custom-call | tf_op jit(solution)/shard_map/scale_update/pallas_call | solution.py:492

commit v4 on v3

--- a/solution.py
+++ b/solution.py
@@ -1,3 +1,5 @@
+import itertools
+
 import jax
 import jax.numpy as jnp
 from jax import lax
@@ -15,31 +17,25 @@
 BF16 = jnp.bfloat16
 SUBS = 8
 LANES = 128
+FORWARD_SEM = (0, 0, 1, 1, 2, 2, 3, 4)
 LAST_STEPS = ((0, 3), (3, 6), (6, 7))
 PLACE = (0, 1, 3, 2)
 
 
 def neighbours():
-    ylo, x, core = (lax.axis_index(a) for a in EXPERT)
-    row, col = lax.axis_index("row"), lax.axis_index("col")
-    group = []
-    for dr in range(2):
-        for dc in range(4):
-            if dr or dc:
-                place = {"row": lax.rem(row + dr, 2), "col": lax.rem(col + dc, 4)}
-                group.append(((dr, dc), place))
-    experts = []
-    for dy in range(2):
-        for dx in range(4):
-            for dk in range(2):
-                if dy or dx or dk:
-                    place = {
-                        "ylo": lax.rem(ylo + dy, 2),
-                        "x": lax.rem(x + dx, 4),
-                        "core": lax.rem(core + dk, 2),
-                    }
-                    experts.append(((dy, dx, dk), place))
-    return dict(group), dict(experts)
+    lengths = (2, 4, 2, 2, 4)
+    axes = (*EXPERT, "row", "col")
+    here = [lax.axis_index(axis) for axis in axes]
+    places = [[lax.rem(at + step, length) for step in range(length)] for at, length in zip(here, lengths)]
+    steps = [s for s in itertools.product(*map(range, lengths)) if any(s)]
+    hops = (1, (0, 1, 2, 1), 0, 2, (0, 1, 2, 1))
+    far = lambda s: sum(h[k] if isinstance(h, tuple) else h * k for h, k in zip(hops, s))
+    steps.sort(key=far, reverse=True)
+    return {s: {axis: places[n][s[n]] for n, axis in enumerate(axes) if s[n]} for s in steps}
+
+
+def back(step):
+    return tuple((length - k) % length for k, length in zip(step, (2, 4, 2, 2, 4)))
 
 
 def ring_sum(parts):
@@ -58,8 +54,8 @@
     weights, inputs, cotangents, row_state_in, col_state_in,
     grad, row_scale, col_scale, new_rows, new_cols,
     xg, yg, xt, xt_last, x_send, y_send, w_buf, row_state, col_state,
-    w_acc, squares, row_base, row_rate, row_part, col_part, row_vec, col_vec, small,
-    ring_rows, pair_cols, group_small, group_total, expert_total, update_part, group_update,
+    w_acc, squares, row_base, row_rate, row_part, col_part, row_vec, col_vec, early, sent,
+    ring_rows, pair_cols, group_early, gathered,
     local_sem, w_sem, send_sem, yz_recv, xz_recv, fw_recv, cross_recv, sum_recv,
 ):
     tokens = inputs.shape[1]
@@ -67,7 +63,10 @@
     half, pair = rows // 2, 2 * tokens
     sub = half // SUBS
     row, col = lax.axis_index("row"), lax.axis_index("col")
-    group, experts = neighbours()
+    everyone = neighbours()
+    group = {key[3:]: device for key, device in everyone.items() if not any(key[:3])}
+    peers = list(group)
+    greeted = [device for key, device in everyone.items() if not any(key[:3]) or not any(key[3:])]
     up, down, across = group[(0, 1)], group[(0, 3)], group[(0, 2)]
     partner = group[(1, 0)]
 
@@ -110,10 +109,9 @@
     w_load(0, 0).start()
 
     barrier = pltpu.get_barrier_semaphore()
-    everyone = [*group.values(), *experts.values()]
-    for device in everyone:
+    for device in greeted:
         pl.semaphore_signal(barrier, inc=1, device_id=device, device_id_type=MESH)
-    pl.semaphore_wait(barrier, len(everyone))
+    pl.semaphore_wait(barrier, len(greeted))
 
     y_copies = []
     for n, (dc, device) in enumerate(zip(y_dest, (up, down, across))):
@@ -126,29 +124,29 @@
         device, j = ((up, 3), (down, 1))[direction]
         width = (lower, upper)[direction ^ part]
         recv = xz_recv.at[s * 2 + part]
-        return remote(tokens_of(xg, 0, s, width), tokens_of(xg, j, s, width), send_sem.at[1], recv, device)
+        return remote(tokens_of(xg, 0, s, width), tokens_of(xg, j, s, width), send_sem.at[0], recv, device)
 
     def forward(s, direction, step):
         device, j = ((up, 3), (down, 1))[direction]
         width = pl.ds(direction * half + step * sub, sub)
         return remote(
-            tokens_of(xg, j, s, width), tokens_of(xg, 2, s, width), send_sem.at[2], fw_recv.at[step], device
+            tokens_of(xg, j, s, width), tokens_of(xg, 2, s, width), send_sem.at[0], fw_recv.at[FORWARD_SEM[step]], device
         )
 
     def await_bytes(like, sem):
         pltpu.make_async_copy(like, like, sem).wait()
 
-    cross_x = remote(x_send, tokens_of(xg, 0, 1), send_sem.at[3], cross_recv.at[4], partner)
+    cross_x = remote(x_send, tokens_of(xg, 0, 1), send_sem.at[0], cross_recv.at[2], partner)
     cross_y = {
-        j: remote(tokens_of(yg, j, 0), tokens_of(yg, j, 1), send_sem.at[4], cross_recv.at[j], partner) for j in (0, 1, 3)
+        j: remote(tokens_of(yg, j, 0), tokens_of(yg, j, 1), send_sem.at[0], cross_recv.at[j], partner) for j in (0, 1, 3)
     }
     n_width = 2 * LANES
     n_steps = cols // n_width
     cross_last = []
     for n, (first, end) in enumerate(LAST_STEPS):
         width = pl.ds(first * n_width, (end - first) * n_width)
-        recv = cross_recv.at[5 + n]
-        cross_last.append(remote(tokens_of(yg, 2, 0, width), tokens_of(yg, 2, 1, width), send_sem.at[4], recv, partner))
+        recv = cross_recv.at[4 + n]
+        cross_last.append(remote(tokens_of(yg, 2, 0, width), tokens_of(yg, 2, 1, width), send_sem.at[0], recv, partner))
 
     loads[0].wait()
     y_copies[0].start()
@@ -187,11 +185,14 @@
     weight_part = w_acc[:, :LANES]
     for n in range(1, cols // LANES):
         weight_part += w_acc[:, n * LANES : (n + 1) * LANES]
-    small[8:16] = weight_part
+    early[0:1] = jnp.sum(weight_part, axis=0, keepdims=True)
     loads[6].wait()
     loads[7].wait()
     old_rows = row_state[...]
-    small[16:24] = old_rows[:8] + old_rows[8:]
+    early[1:2] = jnp.sum(old_rows, axis=0, keepdims=True)
+    for dr, dc in peers:
+        n = dr * 4 + dc - 1
+        remote(early, group_early.at[n], send_sem.at[1], sum_recv.at[0], group[(dr, (4 - dc) % 4)]).start()
 
     def turn(first, count, start, width):
         @pl.loop(0, width // LANES)
@@ -249,14 +250,15 @@
     last = slice(PLACE[2] * pair, (PLACE[2] + 1) * pair)
     lanes = [slice(n * LANES, (n + 1) * LANES) for n in range(cols // LANES)]
 
-    def await_forward(step):
-        await_bytes(x_send.at[:, pl.ds(0, 4 * sub)], fw_recv.at[step])
-        for direction in range(2):
-            at = direction * half + step * sub
-            to = (2 * step + direction) * sub
-            xt_last[to : to + sub, :] = xg[last, at : at + sub].T
-
-    def finish(first, end, steps):
+    def await_forward(*steps):
+        await_bytes(x_send.at[:, pl.ds(0, 4 * sub * len(steps))], fw_recv.at[FORWARD_SEM[steps[0]]])
+        for step in steps:
+            for direction in range(2):
+                at = direction * half + step * sub
+                to = (2 * step + direction) * sub
+                xt_last[to : to + sub, :] = xg[last, at : at + sub].T
+
+    def finish(first, end, steps, row_sums=False):
         for n in range(*steps):
             at = slice(n * n_width, (n + 1) * n_width)
             part = jnp.dot(xt_last[first * 2 * sub : end * 2 * sub], yg[last, at], preferred_element_type=F32)
@@ -269,84 +271,77 @@
                     grad[here, at] = block
                     block = block * block
                     total += jnp.sum(block.reshape(sub // 8, 8, n_width), axis=0)
+                    if row_sums:
+                        block = block[:, :LANES] + block[:, LANES:]
+                        row_part[here] = block if n == 0 else row_part[here] + block
             col_part[:, at] = total
 
-    def square(first, width):
+    def sum_rows(first, end):
         for direction in range(2):
 
-            @pl.loop(0, width // 32)
+            @pl.loop(first * sub // 32, end * sub // 32)
             def _(i):
                 for k in range(4):
-                    begin = direction * half + first + i * 32 + k * 8
-                    here = pl.ds(pl.multiple_of(begin, 8), 8)
-                    line = None
-                    for lane in lanes:
+                    here = pl.ds(pl.multiple_of(direction * half + i * 32 + k * 8, 8), 8)
+                    sums = [None, None]
+                    for n, lane in enumerate(lanes):
                         block = grad[here, lane]
                         block = block * block
-                        squares[here, lane] = block
-                        line = block if line is None else line + block
-                    row_part[here] = line
-
-            for n in range(width // LANES):
-                begin = direction * half + first + n * LANES
-                turned = row_part[begin : begin + LANES].T
-                row_vec[begin // LANES : begin // LANES + 1] = jnp.sum(turned, axis=0, keepdims=True)
-
-    await_forward(0)
-    await_forward(1)
+                        sums[n % 2] = block if sums[n % 2] is None else sums[n % 2] + block
+                    row_part[here] = sums[0] + sums[1]
+
+    def turn_sums():
+        for n in range(rows // LANES):
+            turned = row_part[n * LANES : (n + 1) * LANES].T
+            row_vec[n : n + 1] = jnp.sum(turned, axis=0, keepdims=True)
+
+    def square():
+        @pl.loop(0, rows // 32)
+        def _(i):
+            here = pl.ds(pl.multiple_of(i * 32, 32), 32)
+            block = grad[here, :]
+            squares[here, :] = block * block
+
+    await_forward(0, 1)
     cross_last[0].wait_recv()
     finish(0, 2, LAST_STEPS[0])
-    await_forward(2)
-    await_forward(3)
+    await_forward(2, 3)
     finish(2, 4, LAST_STEPS[0])
     cross_last[1].wait_recv()
     finish(0, 4, LAST_STEPS[1])
-    await_forward(4)
-    await_forward(5)
+    await_forward(4, 5)
     finish(4, 6, (0, LAST_STEPS[1][1]))
     cross_last[2].wait_recv()
     finish(0, 6, LAST_STEPS[2])
     await_forward(6)
-    finish(6, 7, (0, n_steps))
-    square(0, 2 * sub)
+    finish(6, 7, (0, n_steps), row_sums=True)
     await_forward(7)
-    finish(7, 8, (0, n_steps))
+    finish(7, 8, (0, n_steps), row_sums=True)
 
     square_part = col_part[:, :LANES]
     for lane in lanes[1:]:
         square_part += col_part[:, lane]
-    small[0:8] = square_part
-    peers = list(group)
-    for dr, dc in peers:
-        n = dr * 4 + dc - 1
-        remote(small, group_small.at[n], send_sem.at[5], sum_recv.at[0], group[(dr, (4 - dc) % 4)]).start()
+    square_part = jnp.sum(square_part, axis=0, keepdims=True)
+    sent[0] = square_part
+    for n, key in enumerate(everyone):
+        remote(sent.at[0], gathered.at[n], send_sem.at[2], sum_recv.at[3], everyone[back(key)]).start()
+    sum_rows(0, 6)
+    turn_sums()
+    for dc in (1, 2, 3):
+        remote(row_vec, ring_rows.at[dc - 1], send_sem.at[4], sum_recv.at[1], group[(0, (4 - dc) % 4)]).start()
     col_vec[...] = jnp.sum(col_part[...], axis=0, keepdims=True)
-    square(2 * sub, 6 * sub)
-    for dc in (1, 2, 3):
-        remote(row_vec, ring_rows.at[dc - 1], send_sem.at[6], sum_recv.at[1], group[(0, (4 - dc) % 4)]).start()
-    pair_copy = remote(col_vec, pair_cols, send_sem.at[7], sum_recv.at[2], partner)
+    pair_copy = remote(col_vec, pair_cols, send_sem.at[3], sum_recv.at[2], partner)
     pair_copy.start()
-    await_bytes(group_small, sum_recv.at[0])
-
-    def of_group(part):
-        parts = {(0, 0): small[part * 8 : part * 8 + 8]}
-        for dr, dc in peers:
-            parts[(dr, dc)] = group_small[dr * 4 + dc - 1, part * 8 : part * 8 + 8]
-        return parts
-
-    square_part = group_sum(of_group(0))
-    group_total[...] = square_part
-    for n, (dy, dx, dk) in enumerate(experts):
-        remote(
-            group_total, expert_total.at[n], send_sem.at[8], sum_recv.at[3], experts[(dy, (4 - dx) % 4, dk)]
-        ).start()
+    square()
     model_width, hidden_width = 2 * rows, 4 * cols
     entries = model_width * hidden_width
-    matrices = 1 + len(experts)
-    weight_total = full_sum(group_sum(of_group(1)))
-    old = of_group(2)
-    old_total = full_sum(old[(0, 0)] + old[(1, 0)])
-    group_squares = full_sum(square_part)
+    matrices = (1 + len(everyone)) // (1 + len(peers))
+    await_bytes(group_early, sum_recv.at[0])
+    early_parts = {(0, 0): early[...]}
+    for dr, dc in peers:
+        early_parts[(dr, dc)] = group_early[dr * 4 + dc - 1]
+    weight_total = full_sum(group_sum(early_parts)[0:1])
+    old_total = full_sum((early_parts[(0, 0)] + early_parts[(1, 0)])[1:2])
     await_bytes(ring_rows, sum_recv.at[1])
     pair_copy.wait_recv()
     row_total = ring_sum([row_vec[...], ring_rows[0], ring_rows[1], ring_rows[2]])
@@ -357,15 +352,19 @@
         here = slice(n * LANES, (n + 1) * LANES)
         row_base[here] = jnp.broadcast_to(base[n : n + 1], (LANES, LANES)).T
         row_rate[here] = jnp.broadcast_to(rate[n : n + 1], (LANES, LANES)).T
-    await_bytes(expert_total, sum_recv.at[3])
-    totals = {(0, 0, 0): square_part}
-    for n, key in enumerate(experts):
-        totals[key] = expert_total[n]
-    chips = [[totals[(dy, dx, 0)] + totals[(dy, dx, 1)] for dx in range(4)] for dy in range(2)]
+    await_bytes(gathered.at[pl.ds(0, len(everyone))], sum_recv.at[3])
+    parts = {(0, 0, 0, 0, 0): square_part}
+    for n, key in enumerate(everyone):
+        parts[key] = gathered[n]
+    groups = {}
+    for expert in itertools.product(range(2), range(4), range(2)):
+        groups[expert] = group_sum({key[3:]: part for key, part in parts.items() if key[:3] == expert})
+    chips = [[groups[(dy, dx, 0)] + groups[(dy, dx, 1)] for dx in range(4)] for dy in range(2)]
     squared_total = full_sum(ring_sum(chips[0]) + ring_sum(chips[1]))
+    group_squares = full_sum(groups[(0, 0, 0)])
     clip = 1.0 / jnp.maximum(1.0, jnp.sqrt(squared_total / (matrices * entries)))
     clip_square = clip * clip
-    one = clip_square[:1, :1]
+    one = clip_square[:, :1]
     fresh_cols = col_total * one + model_width * EPS
     cols_now = DECAY * col_state[...] + (1.0 - DECAY) * (fresh_cols / model_width)
     col_scale[...] = 1.0 / cols_now
@@ -379,10 +378,13 @@
         line = line / (row_base[here] + row_rate[here] * one)
         return total + jnp.sum(line.reshape(8, 8, LANES), axis=0)
 
-    update_part[...] = lax.fori_loop(0, rows // 64, weigh, jnp.zeros((8, LANES), F32))
+    update_part = lax.fori_loop(0, rows // 64, weigh, jnp.zeros((8, LANES), F32), unroll=2)
+    update_part = jnp.sum(update_part, axis=0, keepdims=True)
+    sent[1] = update_part
+    first = len(everyone)
     for dr, dc in peers:
-        n = dr * 4 + dc - 1
-        remote(update_part, group_update.at[n], send_sem.at[9], sum_recv.at[4], group[(dr, (4 - dc) % 4)]).start()
+        n = first + dr * 4 + dc - 1
+        remote(sent.at[1], gathered.at[n], send_sem.at[2], sum_recv.at[5], group[(dr, (4 - dc) % 4)]).start()
     new_rows[...] = base + rate * one
     new_cols[...] = cols_now
     average = DECAY * (old_total / model_width) + (1.0 - DECAY) * (group_squares * clip_square / entries + EPS)
@@ -394,23 +396,19 @@
 
     col_root = jnp.sqrt(col_scale[...])
     scale = clip * jnp.sqrt(average) * jnp.sqrt(weight_total / entries)
-    await_bytes(y_send, send_sem.at[0])
-    await_bytes(xg.at[pl.ds(0, 4 * tokens)], send_sem.at[1])
-    await_bytes(xg.at[pl.ds(0, 2 * tokens)], send_sem.at[2])
-    cross_x.wait_send()
-    await_bytes(yg.at[pl.ds(0, 4 * tokens)], send_sem.at[4])
-    await_bytes(group_small, send_sem.at[5])
-    await_bytes(ring_rows, send_sem.at[6])
+    sent_bytes = (5 * tokens * rows + 2 * tokens * rows + 7 * tokens * cols) * 2
+    await_bytes(squares.at[pl.ds(0, sent_bytes // (4 * cols))], send_sem.at[0])
+    await_bytes(group_early, send_sem.at[1])
+    await_bytes(ring_rows, send_sem.at[4])
     pair_copy.wait_send()
-    await_bytes(expert_total, send_sem.at[8])
-    await_bytes(group_update, send_sem.at[9])
-    await_bytes(group_update, sum_recv.at[4])
-    parts = {(0, 0): update_part[...]}
+    await_bytes(gathered, send_sem.at[2])
+    await_bytes(gathered.at[pl.ds(first, len(peers))], sum_recv.at[5])
+    parts = {(0, 0): update_part}
     for dr, dc in peers:
-        parts[(dr, dc)] = group_update[dr * 4 + dc - 1]
+        parts[(dr, dc)] = gathered[first + dr * 4 + dc - 1]
     update_total = full_sum(group_sum(parts)) * clip_square * average
     factor = scale / jnp.maximum(1.0, jnp.sqrt(update_total / entries))
-    col_scale[...] = col_root * factor[:1, :1]
+    col_scale[...] = col_root * factor[:, :1]
 
 
 def scale_kernel(grad, row_scale, col_scale, rows_in, cols_in, out, rows_out, cols_out, scaled, sem):
@@ -476,15 +474,13 @@
             pltpu.VMEM((8, cols), F32),
             pltpu.VMEM((lines, LANES), F32),
             pltpu.VMEM((1, cols), F32),
-            pltpu.VMEM((24, LANES), F32),
+            pltpu.VMEM((2, LANES), F32),
+            pltpu.VMEM((2, 1, LANES), F32),
             pltpu.VMEM((3, lines, LANES), F32),
             pltpu.VMEM((1, cols), F32),
-            pltpu.VMEM((7, 24, LANES), F32),
-            pltpu.VMEM((8, LANES), F32),
-            pltpu.VMEM((15, 8, LANES), F32),
-            pltpu.VMEM((8, LANES), F32),
-            pltpu.VMEM((7, 8, LANES), F32),
-            dma((8,)), dma((2,)), dma((10,)), dma((3,)), dma((4,)), dma((SUBS,)), dma((8,)), dma((5,)),
+            pltpu.VMEM((7, 2, LANES), F32),
+            pltpu.VMEM((134, 1, LANES), F32),
+            dma((8,)), dma((2,)), dma((5,)), dma((3,)), dma((4,)), dma((5,)), dma((7,)), dma((6,)),
         ],
         compiler_params=pltpu.CompilerParams(collective_id=0, has_side_effects=True, vmem_limit_bytes=40 * 2**20),
         cost_estimate=pl.CostEstimate(flops=16 * tokens * rows * cols, bytes_accessed=2**23, transcendentals=0),

time: 87.8 us -> 83.7 us (0.953)
  Pallas kernels: 86.4 us -> 82.6 us
    pallas_call x1, Pallas kernels: 81.1 us -> 77.4 us  [body(): pl.pallas_call(gather_kernel, name='gather_gradient', out_shape=shapes, i...]
where the time goes in v4:
time: 83.7 us; the launch traced here: 83.4 us
  Pallas kernels  82.6 us (99%)
    pallas_call x1, Pallas kernels, body(): pl.pallas_call(gather_kernel, name='gather_gradient', out_shape=shapes, i...  77.4 us
    pallas_call x1, Pallas kernels, body(): pl.pallas_call(scale_kernel, name='scale_update', out_shape=[jax.ShapeDty...  5.26 us

profile of v4, /device:TPU:0, one launch (start us, length us, event | category | flops | bytes accessed | tf_op | source)
XLA Modules:
  0.0 83.4 jit_solution(7806856148130179022)
XLA Ops:
  0.6 77.4 %gather_gradient.1 = (f32[2048,1792]{1,0:T(8,128)S(1)}, f32[2048,128]{1,0:T(8,128)S(1)}, f32[1,1792]{1,0:T(1,128)S(1)}, f32[16,128]{1,0:T(8,128)S(1)}, f32[1,1792]{1,0:T(1,128)S(1)}) custom-call(bf16[1,2048,1792]{2,1,0:T(8,128)(2,1)} %weights.1, bf16[1,128,4096]{2,1,0:T(8,128)(2,1)} %inputs.1, bf16[1,128,7168]{2,1,0:T(8,128)(2,1)} %cotangents.1, ...), custom_call_target="tpu_custom_call" | custom-call | flops 7516192768 | bytes 8388608 | tf_op jit(solution)/shard_map/gather_gradient/pallas_call | solution.py:453
  78.0 5.3 %scale_update.1 = (f32[2048,1792]{1,0:T(8,128)}, f32[16,128]{1,0:T(8,128)}, f32[1,1792]{1,0:T(1,128)}) custom-call(f32[2048,1792]{1,0:T(8,128)S(1)} %get-tuple-element.11.grad, f32[2048,128]{1,0:T(8,128)S(1)} %get-tuple-element.12.row_scale, f32[1,1792]{1,0:T(1,128)S(1)} %get-tuple-element.13.col_scale, f32[16,128]{1,0:T(8,128)S(1)} %get-tuple-element.14.rows_in, ...), custom_call_target="tpu_custom_call" | custom-call | tf_op jit(solution)/shard_map/scale_update/pallas_call | solution.py:488

commit v5 on v4

--- a/solution.py
+++ b/solution.py
@@ -17,7 +17,7 @@
 BF16 = jnp.bfloat16
 SUBS = 8
 LANES = 128
-FORWARD_SEM = (0, 0, 1, 1, 2, 2, 3, 4)
+FORWARD_SEM = (0, 0, 1, 1, 2, 3, 4, 5)
 LAST_STEPS = ((0, 3), (3, 6), (6, 7))
 PLACE = (0, 1, 3, 2)
 
@@ -116,14 +116,14 @@
     y_copies = []
     for n, (dc, device) in enumerate(zip(y_dest, (up, down, across))):
         y_copies.append(
-            remote(y_send.at[n], tokens_of(yg, (4 - dc) % 4, 0), send_sem.at[0], yz_recv.at[n], device)
+            remote(y_send.at[n], tokens_of(yg, (4 - dc) % 4, 0), send_sem.at[0], yz_recv.at[n // 2], device)
         )
     lower, upper = pl.ds(0, half), pl.ds(half, half)
 
     def x_copy(s, direction, part):
         device, j = ((up, 3), (down, 1))[direction]
         width = (lower, upper)[direction ^ part]
-        recv = xz_recv.at[s * 2 + part]
+        recv = xz_recv.at[part]
         return remote(tokens_of(xg, 0, s, width), tokens_of(xg, j, s, width), send_sem.at[0], recv, device)
 
     def forward(s, direction, step):
@@ -213,8 +213,7 @@
                     part += grad[here, at]
                 grad[here, at] = part
 
-    y_copies[0].wait_recv()
-    y_copies[1].wait_recv()
+    await_bytes(yg.at[pl.ds(0, 2 * tokens)], yz_recv.at[0])
     cross_y[3].start()
     cross_y[1].start()
     cross_x.wait_recv()
@@ -228,8 +227,7 @@
     for copy in cross_last:
         copy.start()
 
-    await_bytes(x_send, xz_recv.at[0])
-    await_bytes(x_send, xz_recv.at[2])
+    await_bytes(xg.at[pl.ds(0, 2 * tokens)], xz_recv.at[0])
     for step in range(SUBS):
         for s in range(2):
             for direction in range(2):
@@ -240,8 +238,7 @@
     multiply(2, (0,))
     cross_y[1].wait_recv()
     multiply(1, (1,))
-    await_bytes(x_send, xz_recv.at[1])
-    await_bytes(x_send, xz_recv.at[3])
+    await_bytes(xg.at[pl.ds(0, 2 * tokens)], xz_recv.at[1])
     turn(2, 1, half, half)
     turn(1, 1, 0, half)
     multiply(2, (1,))
@@ -258,42 +255,31 @@
                 to = (2 * step + direction) * sub
                 xt_last[to : to + sub, :] = xg[last, at : at + sub].T
 
-    def finish(first, end, steps, row_sums=False):
+    def finish(first, end, steps):
         for n in range(*steps):
             at = slice(n * n_width, (n + 1) * n_width)
-            part = jnp.dot(xt_last[first * 2 * sub : end * 2 * sub], yg[last, at], preferred_element_type=F32)
             total = col_part[:, at]
             for step in range(first, end):
                 for direction in range(2):
                     here = slice(direction * half + step * sub, direction * half + (step + 1) * sub)
                     begin = (2 * (step - first) + direction) * sub
-                    block = part[begin : begin + sub] + grad[here, at]
+                    place = first * 2 * sub + begin
+                    block = grad[here, at] + jnp.dot(
+                        xt_last[place : place + sub], yg[last, at], preferred_element_type=F32
+                    )
                     grad[here, at] = block
                     block = block * block
                     total += jnp.sum(block.reshape(sub // 8, 8, n_width), axis=0)
-                    if row_sums:
-                        block = block[:, :LANES] + block[:, LANES:]
-                        row_part[here] = block if n == 0 else row_part[here] + block
+                    block = block[:, :LANES] + block[:, LANES:]
+                    row_part[here] = block if n == 0 else row_part[here] + block
             col_part[:, at] = total
 
-    def sum_rows(first, end):
+    def turn_sums(first, end):
         for direction in range(2):
-
-            @pl.loop(first * sub // 32, end * sub // 32)
-            def _(i):
-                for k in range(4):
-                    here = pl.ds(pl.multiple_of(direction * half + i * 32 + k * 8, 8), 8)
-                    sums = [None, None]
-                    for n, lane in enumerate(lanes):
-                        block = grad[here, lane]
-                        block = block * block
-                        sums[n % 2] = block if sums[n % 2] is None else sums[n % 2] + block
-                    row_part[here] = sums[0] + sums[1]
-
-    def turn_sums():
-        for n in range(rows // LANES):
-            turned = row_part[n * LANES : (n + 1) * LANES].T
-            row_vec[n : n + 1] = jnp.sum(turned, axis=0, keepdims=True)
+            for step in range(first, end):
+                begin = direction * half + step * sub
+                turned = row_part[begin : begin + sub].T
+                row_vec[begin // LANES : begin // LANES + 1] = jnp.sum(turned, axis=0, keepdims=True)
 
     def square():
         @pl.loop(0, rows // 32)
@@ -309,14 +295,17 @@
     finish(2, 4, LAST_STEPS[0])
     cross_last[1].wait_recv()
     finish(0, 4, LAST_STEPS[1])
-    await_forward(4, 5)
-    finish(4, 6, (0, LAST_STEPS[1][1]))
+    await_forward(4)
+    finish(4, 5, (0, LAST_STEPS[1][1]))
     cross_last[2].wait_recv()
-    finish(0, 6, LAST_STEPS[2])
+    finish(0, 5, LAST_STEPS[2])
+    await_forward(5)
+    finish(5, 6, (0, n_steps))
     await_forward(6)
-    finish(6, 7, (0, n_steps), row_sums=True)
+    finish(6, 7, (0, n_steps))
+    turn_sums(0, 6)
     await_forward(7)
-    finish(7, 8, (0, n_steps), row_sums=True)
+    finish(7, 8, (0, n_steps))
 
     square_part = col_part[:, :LANES]
     for lane in lanes[1:]:
@@ -325,8 +314,7 @@
     sent[0] = square_part
     for n, key in enumerate(everyone):
         remote(sent.at[0], gathered.at[n], send_sem.at[2], sum_recv.at[3], everyone[back(key)]).start()
-    sum_rows(0, 6)
-    turn_sums()
+    turn_sums(6, 8)
     for dc in (1, 2, 3):
         remote(row_vec, ring_rows.at[dc - 1], send_sem.at[4], sum_recv.at[1], group[(0, (4 - dc) % 4)]).start()
     col_vec[...] = jnp.sum(col_part[...], axis=0, keepdims=True)
@@ -480,7 +468,7 @@
             pltpu.VMEM((1, cols), F32),
             pltpu.VMEM((7, 2, LANES), F32),
             pltpu.VMEM((134, 1, LANES), F32),
-            dma((8,)), dma((2,)), dma((5,)), dma((3,)), dma((4,)), dma((5,)), dma((7,)), dma((6,)),
+            dma((8,)), dma((2,)), dma((5,)), dma((2,)), dma((2,)), dma((6,)), dma((7,)), dma((6,)),
         ],
         compiler_params=pltpu.CompilerParams(collective_id=0, has_side_effects=True, vmem_limit_bytes=40 * 2**20),
         cost_estimate=pl.CostEstimate(flops=16 * tokens * rows * cols, bytes_accessed=2**23, transcendentals=0),

time: 83.7 us -> 82 us (0.980)
  Pallas kernels: 82.6 us -> 81.2 us
    pallas_call x1, Pallas kernels: 77.4 us -> 75.9 us  [body(): pl.pallas_call(gather_kernel, name='gather_gradient', out_shape=shapes, i...]
where the time goes in v5:
time: 82 us; the launch traced here: 81.8 us
  Pallas kernels  81.2 us (99%)
    pallas_call x1, Pallas kernels, body(): pl.pallas_call(gather_kernel, name='gather_gradient', out_shape=shapes, i...  75.9 us
    pallas_call x1, Pallas kernels, body(): pl.pallas_call(scale_kernel, name='scale_update', out_shape=[jax.ShapeDty...  5.26 us

profile of v5, /device:TPU:0, one launch (start us, length us, event | category | flops | bytes accessed | tf_op | source)
XLA Modules:
  0.0 81.8 jit_solution(15994206983883559582)
XLA Ops:
  0.6 75.9 %gather_gradient.1 = (f32[2048,1792]{1,0:T(8,128)S(1)}, f32[2048,128]{1,0:T(8,128)S(1)}, f32[1,1792]{1,0:T(1,128)S(1)}, f32[16,128]{1,0:T(8,128)S(1)}, f32[1,1792]{1,0:T(1,128)S(1)}) custom-call(bf16[1,2048,1792]{2,1,0:T(8,128)(2,1)} %weights.1, bf16[1,128,4096]{2,1,0:T(8,128)(2,1)} %inputs.1, bf16[1,128,7168]{2,1,0:T(8,128)(2,1)} %cotangents.1, ...), custom_call_target="tpu_custom_call" | custom-call | flops 7516192768 | bytes 8388608 | tf_op jit(solution)/shard_map/gather_gradient/pallas_call | solution.py:441
  76.5 5.3 %scale_update.1 = (f32[2048,1792]{1,0:T(8,128)}, f32[16,128]{1,0:T(8,128)}, f32[1,1792]{1,0:T(1,128)}) custom-call(f32[2048,1792]{1,0:T(8,128)S(1)} %get-tuple-element.11.grad, f32[2048,128]{1,0:T(8,128)S(1)} %get-tuple-element.12.row_scale, f32[1,1792]{1,0:T(1,128)S(1)} %get-tuple-element.13.col_scale, f32[16,128]{1,0:T(8,128)S(1)} %get-tuple-element.14.rows_in, ...), custom_call_target="tpu_custom_call" | custom-call | tf_op jit(solution)/shard_map/scale_update/pallas_call | solution.py:476

commit v6 on v5

--- a/solution.py
+++ b/solution.py
@@ -17,6 +17,7 @@
 BF16 = jnp.bfloat16
 SUBS = 8
 LANES = 128
+LOCAL_SEM = (0, 0, 1, 2, 3, 1)
 FORWARD_SEM = (0, 0, 1, 1, 2, 3, 4, 5)
 LAST_STEPS = ((0, 3), (3, 6), (6, 7))
 PLACE = (0, 1, 3, 2)
@@ -66,7 +67,8 @@
     everyone = neighbours()
     group = {key[3:]: device for key, device in everyone.items() if not any(key[:3])}
     peers = list(group)
-    greeted = [device for key, device in everyone.items() if not any(key[:3]) or not any(key[3:])]
+    near = {(0, 1), (0, 2), (0, 3), (1, 0)}
+    greeted = [device for key, device in everyone.items() if not any(key[3:]) or not any(key[:3]) and key[3:] in near]
     up, down, across = group[(0, 1)], group[(0, 3)], group[(0, 2)]
     partner = group[(1, 0)]
 
@@ -94,9 +96,9 @@
     local.append((inputs.at[0, :, row_cols(1 - row)], x_send))
     local.append((inputs.at[0, :, row_cols(row)], tokens_of(xg, 0, 0)))
     local.append((cotangents.at[0, :, col_cols(col)], tokens_of(yg, 0, 0)))
-    loads = [pltpu.make_async_copy(s, d, local_sem.at[n]) for n, (s, d) in enumerate(local)]
-    loads.append(pltpu.make_async_copy(row_state_in, row_state, local_sem.at[6]))
-    loads.append(pltpu.make_async_copy(col_state_in, col_state, local_sem.at[7]))
+    loads = [pltpu.make_async_copy(s, d, local_sem.at[LOCAL_SEM[n]]) for n, (s, d) in enumerate(local)]
+    loads.append(pltpu.make_async_copy(row_state_in, row_state, local_sem.at[4]))
+    loads.append(pltpu.make_async_copy(col_state_in, col_state, local_sem.at[5]))
     for n in (0, 1, 3, 4, 5, 2, 6, 7):
         loads[n].start()
     w_rows = w_buf.shape[1]
@@ -148,9 +150,8 @@
         recv = cross_recv.at[4 + n]
         cross_last.append(remote(tokens_of(yg, 2, 0, width), tokens_of(yg, 2, 1, width), send_sem.at[0], recv, partner))
 
-    loads[0].wait()
+    await_bytes(y_send.at[pl.ds(0, 2)], local_sem.at[0])
     y_copies[0].start()
-    loads[1].wait()
     y_copies[1].start()
     loads[3].wait()
     cross_x.start()
@@ -158,9 +159,8 @@
     for part in range(2):
         for direction in range(2):
             x_copy(0, direction, part).start()
-    loads[5].wait()
+    await_bytes(y_send.at[pl.ds(0, 2)], local_sem.at[1])
     cross_y[0].start()
-    loads[2].wait()
     y_copies[2].start()
 
     w_acc[...] = jnp.zeros_like(w_acc)
@@ -190,9 +190,6 @@
     loads[7].wait()
     old_rows = row_state[...]
     early[1:2] = jnp.sum(old_rows, axis=0, keepdims=True)
-    for dr, dc in peers:
-        n = dr * 4 + dc - 1
-        remote(early, group_early.at[n], send_sem.at[1], sum_recv.at[0], group[(dr, (4 - dc) % 4)]).start()
 
     def turn(first, count, start, width):
         @pl.loop(0, width // LANES)
@@ -298,6 +295,9 @@
     await_forward(4)
     finish(4, 5, (0, LAST_STEPS[1][1]))
     cross_last[2].wait_recv()
+    for dr, dc in peers:
+        n = dr * 4 + dc - 1
+        remote(early, group_early.at[n], send_sem.at[1], sum_recv.at[0], group[(dr, (4 - dc) % 4)]).start()
     finish(0, 5, LAST_STEPS[2])
     await_forward(5)
     finish(5, 6, (0, n_steps))
@@ -350,8 +350,7 @@
     chips = [[groups[(dy, dx, 0)] + groups[(dy, dx, 1)] for dx in range(4)] for dy in range(2)]
     squared_total = full_sum(ring_sum(chips[0]) + ring_sum(chips[1]))
     group_squares = full_sum(groups[(0, 0, 0)])
-    clip = 1.0 / jnp.maximum(1.0, jnp.sqrt(squared_total / (matrices * entries)))
-    clip_square = clip * clip
+    clip_square = 1.0 / jnp.maximum(1.0, squared_total / (matrices * entries))
     one = clip_square[:, :1]
     fresh_cols = col_total * one + model_width * EPS
     cols_now = DECAY * col_state[...] + (1.0 - DECAY) * (fresh_cols / model_width)
@@ -383,7 +382,7 @@
         row_scale[here] = 1.0 / jnp.sqrt(row_base[here] + row_rate[here] * one)
 
     col_root = jnp.sqrt(col_scale[...])
-    scale = clip * jnp.sqrt(average) * jnp.sqrt(weight_total / entries)
+    scale = jnp.sqrt(clip_square) * jnp.sqrt(average) * jnp.sqrt(weight_total / entries)
     sent_bytes = (5 * tokens * rows + 2 * tokens * rows + 7 * tokens * cols) * 2
     await_bytes(squares.at[pl.ds(0, sent_bytes // (4 * cols))], send_sem.at[0])
     await_bytes(group_early, send_sem.at[1])
@@ -468,7 +467,7 @@
             pltpu.VMEM((1, cols), F32),
             pltpu.VMEM((7, 2, LANES), F32),
             pltpu.VMEM((134, 1, LANES), F32),
-            dma((8,)), dma((2,)), dma((5,)), dma((2,)), dma((2,)), dma((6,)), dma((7,)), dma((6,)),
+            dma((6,)), dma((2,)), dma((5,)), dma((2,)), dma((2,)), dma((6,)), dma((7,)), dma((6,)),
         ],
         compiler_params=pltpu.CompilerParams(collective_id=0, has_side_effects=True, vmem_limit_bytes=40 * 2**20),
         cost_estimate=pl.CostEstimate(flops=16 * tokens * rows * cols, bytes_accessed=2**23, transcendentals=0),

time: 82 us -> 81.9 us (level)
  no operation moved by 1% of the time
where the time goes in v6:
time: 81.9 us; the launch traced here: 81.7 us
  Pallas kernels  80.9 us (99%)
    pallas_call x1, Pallas kernels, body(): pl.pallas_call(gather_kernel, name='gather_gradient', out_shape=shapes, i...  75.6 us
    pallas_call x1, Pallas kernels, body(): pl.pallas_call(scale_kernel, name='scale_update', out_shape=[jax.ShapeDty...  5.26 us

profile of v6, /device:TPU:0, one launch (start us, length us, event | category | flops | bytes accessed | tf_op | source)
XLA Modules:
  0.0 81.7 jit_solution(12200865961377495752)
XLA Ops:
  0.6 75.6 %gather_gradient.1 = (f32[2048,1792]{1,0:T(8,128)S(1)}, f32[2048,128]{1,0:T(8,128)S(1)}, f32[1,1792]{1,0:T(1,128)S(1)}, f32[16,128]{1,0:T(8,128)S(1)}, f32[1,1792]{1,0:T(1,128)S(1)}) custom-call(bf16[1,2048,1792]{2,1,0:T(8,128)(2,1)} %weights.1, bf16[1,128,4096]{2,1,0:T(8,128)(2,1)} %inputs.1, bf16[1,128,7168]{2,1,0:T(8,128)(2,1)} %cotangents.1, ...), custom_call_target="tpu_custom_call" | custom-call | flops 7516192768 | bytes 8388608 | tf_op jit(solution)/shard_map/gather_gradient/pallas_call | solution.py:440
  76.2 5.3 %scale_update.1 = (f32[2048,1792]{1,0:T(8,128)}, f32[16,128]{1,0:T(8,128)}, f32[1,1792]{1,0:T(1,128)}) custom-call(f32[2048,1792]{1,0:T(8,128)S(1)} %get-tuple-element.11.grad, f32[2048,128]{1,0:T(8,128)S(1)} %get-tuple-element.12.row_scale, f32[1,1792]{1,0:T(1,128)S(1)} %get-tuple-element.13.col_scale, f32[16,128]{1,0:T(8,128)S(1)} %get-tuple-element.14.rows_in, ...), custom_call_target="tpu_custom_call" | custom-call | tf_op jit(solution)/shard_map/scale_update/pallas_call | solution.py:475

commit v7 on v6

--- a/solution.py
+++ b/solution.py
@@ -287,6 +287,9 @@
 
     await_forward(0, 1)
     cross_last[0].wait_recv()
+    for dr, dc in peers:
+        n = dr * 4 + dc - 1
+        remote(early, group_early.at[n], send_sem.at[1], sum_recv.at[0], group[(dr, (4 - dc) % 4)]).start()
     finish(0, 2, LAST_STEPS[0])
     await_forward(2, 3)
     finish(2, 4, LAST_STEPS[0])
@@ -295,15 +298,11 @@
     await_forward(4)
     finish(4, 5, (0, LAST_STEPS[1][1]))
     cross_last[2].wait_recv()
-    for dr, dc in peers:
-        n = dr * 4 + dc - 1
-        remote(early, group_early.at[n], send_sem.at[1], sum_recv.at[0], group[(dr, (4 - dc) % 4)]).start()
     finish(0, 5, LAST_STEPS[2])
     await_forward(5)
     finish(5, 6, (0, n_steps))
     await_forward(6)
     finish(6, 7, (0, n_steps))
-    turn_sums(0, 6)
     await_forward(7)
     finish(7, 8, (0, n_steps))
 
@@ -314,7 +313,7 @@
     sent[0] = square_part
     for n, key in enumerate(everyone):
         remote(sent.at[0], gathered.at[n], send_sem.at[2], sum_recv.at[3], everyone[back(key)]).start()
-    turn_sums(6, 8)
+    turn_sums(0, 8)
     for dc in (1, 2, 3):
         remote(row_vec, ring_rows.at[dc - 1], send_sem.at[4], sum_recv.at[1], group[(0, (4 - dc) % 4)]).start()
     col_vec[...] = jnp.sum(col_part[...], axis=0, keepdims=True)

time: 81.9 us -> 81.9 us (level)
  no operation moved by 1% of the time
where the time goes in v7:
time: 81.9 us; the launch traced here: 81.7 us
  Pallas kernels  80.9 us (99%)
    pallas_call x1, Pallas kernels, body(): pl.pallas_call(gather_kernel, name='gather_gradient', out_shape=shapes, i...  75.6 us
    pallas_call x1, Pallas kernels, body(): pl.pallas_call(scale_kernel, name='scale_update', out_shape=[jax.ShapeDty...  5.26 us

profile of v7, /device:TPU:0, one launch (start us, length us, event | category | flops | bytes accessed | tf_op | source)
XLA Modules:
  0.0 81.7 jit_solution(6768820157222488661)
XLA Ops:
  0.6 75.6 %gather_gradient.1 = (f32[2048,1792]{1,0:T(8,128)S(1)}, f32[2048,128]{1,0:T(8,128)S(1)}, f32[1,1792]{1,0:T(1,128)S(1)}, f32[16,128]{1,0:T(8,128)S(1)}, f32[1,1792]{1,0:T(1,128)S(1)}) custom-call(bf16[1,2048,1792]{2,1,0:T(8,128)(2,1)} %weights.1, bf16[1,128,4096]{2,1,0:T(8,128)(2,1)} %inputs.1, bf16[1,128,7168]{2,1,0:T(8,128)(2,1)} %cotangents.1, ...), custom_call_target="tpu_custom_call" | custom-call | flops 7516192768 | bytes 8388608 | tf_op jit(solution)/shard_map/gather_gradient/pallas_call | solution.py:439
  76.3 5.3 %scale_update.1 = (f32[2048,1792]{1,0:T(8,128)}, f32[16,128]{1,0:T(8,128)}, f32[1,1792]{1,0:T(1,128)}) custom-call(f32[2048,1792]{1,0:T(8,128)S(1)} %get-tuple-element.11.grad, f32[2048,128]{1,0:T(8,128)S(1)} %get-tuple-element.12.row_scale, f32[1,1792]{1,0:T(1,128)S(1)} %get-tuple-element.13.col_scale, f32[16,128]{1,0:T(8,128)S(1)} %get-tuple-element.14.rows_in, ...), custom_call_target="tpu_custom_call" | custom-call | tf_op jit(solution)/shard_map/scale_update/pallas_call | solution.py:474
